TPU v7x, 32 devices: a whole 2x2x4 slice. The times are simulated.
32 devices in a mesh: req: 4 (over x, y), dap: 8 (over z, core).
Axes of the slice: x: 2, y: 2, z: 4, core: 2. Of those that a mesh axis runs over, the one named last changes fastest.
Arguments:
- msa_act: bfloat16 [1024, 128, 256], P(('req', 'dap')), parts along dimension 0
- pair_act: bfloat16 [512, 128, 128], P(('req', 'dap')), parts along dimension 0
- msa_mask: int32 [1024, 128], P(('req', 'dap')), parts along dimension 0
- pair_mask: int32 [512, 128], P(('req', 'dap')), parts along dimension 0
- row_qkvg: bfloat16 [2, 256, 1024], replicated
- row_bias: bfloat16 [2, 128, 8], replicated
- row_out: bfloat16 [2, 256, 256], replicated
- col_qkvg: bfloat16 [2, 256, 1024], replicated
- col_out: bfloat16 [2, 256, 256], replicated
- mtr_in: bfloat16 [2, 256, 1024], replicated
- mtr_out: bfloat16 [2, 1024, 256], replicated
- opm_proj: bfloat16 [2, 256, 64], replicated
- opm_out: bfloat16 [2, 1024, 128], replicated
- tmo_proj: bfloat16 [2, 128, 640], replicated
- tmo_out: bfloat16 [2, 128, 128], replicated
- tmi_proj: bfloat16 [2, 128, 640], replicated
- tmi_out: bfloat16 [2, 128, 128], replicated
- tas_qkvg: bfloat16 [2, 128, 512], replicated
- tas_bias: bfloat16 [2, 128, 4], replicated
- tas_out: bfloat16 [2, 128, 128], replicated
- tae_qkvg: bfloat16 [2, 128, 512], replicated
- tae_bias: bfloat16 [2, 128, 4], replicated
- tae_out: bfloat16 [2, 128, 128], replicated
- ptr_in: bfloat16 [2, 128, 512], replicated
- ptr_out: bfloat16 [2, 512, 128], replicated
Outputs:
- output 1: bfloat16 [1024, 128, 256], P(('req', 'dap')), parts along dimension 0
- output 2: bfloat16 [512, 128, 128], P(('req', 'dap')), parts along dimension 0
There are 4 independent parts. A program takes and returns all parts, laid end to end along the dimension named above; an argument that names none is the same for every part.
All inputs are finite; a program needn't handle non-finite values.
Results may differ from a plain program's by a relative error of at most 0.02.
Values are sent between devices in bfloat16 or wider.
A program may use at most 1 GiB of HBM per device.

v0:
```python
import jax
import jax.numpy as jnp
from jax import lax
from jax.sharding import PartitionSpec as P

GROUP_AXIS = 'dap'
PARTS_AXIS = 'req'
MASKED_LOGIT = -1e9


def layer_norm(x):
    values = x.astype(jnp.float32)
    centered = values - jnp.mean(values, axis=-1, keepdims=True)
    variance = jnp.mean(centered * centered, axis=-1, keepdims=True)
    return (centered * lax.rsqrt(variance + 1e-5)).astype(jnp.bfloat16)


def residual(x, update):
    return (x.astype(jnp.float32) + update).astype(jnp.bfloat16)


def dense(x, weight):
    return jnp.einsum('...c,cf->...f', x, weight, preferred_element_type=jnp.float32)


def attend(queries, gate_raw, keyvals, num_heads, pair_bias, key_mask, w_out):
    n_batch, q_len, head_width = queries.shape
    k_len = keyvals.shape[1]
    head_dim = head_width // num_heads
    q_heads = queries.reshape(n_batch, q_len, num_heads, head_dim)
    k_heads = keyvals[..., :head_width].reshape(n_batch, k_len, num_heads, head_dim)
    v_heads = keyvals[..., head_width:].reshape(n_batch, k_len, num_heads, head_dim)
    logits = jnp.einsum('bqhd,bkhd->bhqk', q_heads, k_heads, preferred_element_type=jnp.float32) * head_dim ** -0.5
    if pair_bias is not None:
        logits = logits + pair_bias.astype(jnp.float32)
    logits = jnp.where(key_mask[:, None, None, :] > 0, logits, MASKED_LOGIT)
    attn_prob = jax.nn.softmax(logits, axis=-1).astype(jnp.bfloat16)
    attended = jnp.einsum('bhqk,bkhd->bqhd', attn_prob, v_heads, preferred_element_type=jnp.float32)
    gated = (attended.reshape(n_batch, q_len, head_width) * jax.nn.sigmoid(gate_raw.astype(jnp.float32))).astype(jnp.bfloat16)
    return dense(gated, w_out)


def self_attention(x_norm, w_qkvg, num_heads, pair_bias, key_mask, w_out):
    head_width = w_out.shape[0]
    projected = dense(x_norm, w_qkvg).astype(jnp.bfloat16)
    return attend(projected[..., :head_width], projected[..., 3 * head_width:], projected[..., head_width:3 * head_width], num_heads, pair_bias, key_mask, w_out)


def head_bias(pair_norm, w_bias):
    return jnp.einsum('ijc,ch->hij', pair_norm, w_bias, preferred_element_type=jnp.float32).astype(jnp.bfloat16)


def transition(x, w_in, w_out):
    hidden = jnp.maximum(dense(layer_norm(x), w_in), 0.0).astype(jnp.bfloat16)
    return dense(hidden, w_out)


def outer_update(array_b7, res_mask, full_mask, w_proj, w_out):
    opm_dim = w_proj.shape[1] // 2
    projected = dense(layer_norm(array_b7), w_proj).astype(jnp.bfloat16)
    mask_bf = res_mask.astype(jnp.bfloat16)[:, :, None]
    left_act = projected[..., :opm_dim] * mask_bf
    right_act = projected[..., opm_dim:] * mask_bf
    right_full = lax.all_gather(right_act, GROUP_AXIS, axis=1, tiled=True)
    outer_prod = jnp.einsum('sic,sje->ijce', left_act, right_full, preferred_element_type=jnp.float32).astype(jnp.bfloat16)
    n_rows, n_cols = outer_prod.shape[:2]
    update = dense(outer_prod.reshape(n_rows, n_cols, opm_dim * opm_dim), w_out)
    overlap = jnp.einsum('si,sj->ij', res_mask.astype(jnp.float32), full_mask.astype(jnp.float32))
    return update / (1e-3 + overlap)[:, :, None]


def tri_gates(pair_rows, mask_rows, w_proj):
    tri_dim = (w_proj.shape[1] - pair_rows.shape[-1]) // 4
    projected = dense(layer_norm(pair_rows), w_proj)
    mask_f = mask_rows.astype(jnp.float32)[:, :, None]
    left_act = (mask_f * jax.nn.sigmoid(projected[..., 2 * tri_dim:3 * tri_dim]) * projected[..., :tri_dim]).astype(jnp.bfloat16)
    right_act = (mask_f * jax.nn.sigmoid(projected[..., 3 * tri_dim:4 * tri_dim]) * projected[..., tri_dim:2 * tri_dim]).astype(jnp.bfloat16)
    gate_act = jax.nn.sigmoid(projected[..., 4 * tri_dim:])
    return left_act, right_act, gate_act


def tri_finish(product, gate_act, w_out):
    return gate_act * dense(layer_norm(product), w_out)


def tri_attention(pair_rows, mask_rows, w_qkvg, w_bias, w_out):
    pair_norm = layer_norm(pair_rows)
    bias_full = lax.all_gather(head_bias(pair_norm, w_bias), GROUP_AXIS, axis=1, tiled=True)
    return self_attention(pair_norm, w_qkvg, w_bias.shape[1], bias_full, mask_rows, w_out)


def pair_stack(pair_loc, pair_mask, pair_mask_t, pair_w):
    (tmo_proj, tmo_out, tmi_proj, tmi_out, tas_qkvg, tas_bias, tas_out,
     tae_qkvg, tae_bias, tae_out, ptr_in, ptr_out) = pair_w
    left_act, right_act, gate_act = tri_gates(pair_loc, pair_mask, tmo_proj)
    right_full = lax.all_gather(right_act, GROUP_AXIS, axis=0, tiled=True)
    product = jnp.einsum('ikc,jkc->ijc', left_act, right_full, preferred_element_type=jnp.float32)
    pair_loc = residual(pair_loc, tri_finish(product, gate_act, tmo_out))
    left_act, right_act, gate_act = tri_gates(pair_loc, pair_mask, tmi_proj)
    left_cols = lax.all_to_all(left_act, GROUP_AXIS, 1, 0, tiled=True)
    right_full = lax.all_gather(right_act, GROUP_AXIS, axis=0, tiled=True)
    product = jnp.einsum('kic,kjc->ijc', left_cols, right_full, preferred_element_type=jnp.float32)
    pair_loc = residual(pair_loc, tri_finish(product, gate_act, tmi_out))
    pair_loc = residual(pair_loc, tri_attention(pair_loc, pair_mask, tas_qkvg, tas_bias, tas_out))
    pair_cols = lax.all_to_all(pair_loc, GROUP_AXIS, 1, 0, tiled=True)
    pair_t = jnp.swapaxes(pair_cols, 0, 1)
    pair_t = residual(pair_t, tri_attention(pair_t, pair_mask_t, tae_qkvg, tae_bias, tae_out))
    pair_loc = lax.all_to_all(jnp.swapaxes(pair_t, 0, 1), GROUP_AXIS, 0, 1, tiled=True)
    return residual(pair_loc, transition(pair_loc, ptr_in, ptr_out))


def evoformer_block(value_a7, pair_loc, full_mask, full_pair_mask, layer_w):
    (row_qkvg, row_bias, row_out, col_qkvg, col_out, mtr_in, mtr_out, opm_proj, opm_out) = layer_w[:9]
    shard_idx = lax.axis_index(GROUP_AXIS)
    seq_loc = value_a7.shape[0]
    res_loc = pair_loc.shape[0]
    seq_mask = lax.dynamic_slice_in_dim(full_mask, shard_idx * seq_loc, seq_loc, 0)
    res_mask = lax.dynamic_slice_in_dim(full_mask, shard_idx * res_loc, res_loc, 1)
    pair_mask = lax.dynamic_slice_in_dim(full_pair_mask, shard_idx * res_loc, res_loc, 0)
    pair_mask_t = lax.dynamic_slice_in_dim(full_pair_mask, shard_idx * res_loc, res_loc, 1).T
    value_a9 = row_bias.shape[1]
    row_bias_full = lax.all_gather(head_bias(layer_norm(pair_loc), row_bias), GROUP_AXIS, axis=1, tiled=True)
    value_a7 = residual(value_a7, self_attention(layer_norm(value_a7), row_qkvg, value_a9, row_bias_full, seq_mask, row_out))
    array_b7 = lax.all_to_all(value_a7, GROUP_AXIS, 1, 0, tiled=True)
    col_norm = jnp.swapaxes(layer_norm(array_b7), 0, 1)
    col_update = self_attention(col_norm, col_qkvg, value_a9, None, res_mask.T, col_out)
    array_b7 = residual(array_b7, jnp.swapaxes(col_update, 0, 1))
    array_b7 = residual(array_b7, transition(array_b7, mtr_in, mtr_out))
    pair_loc = residual(pair_loc, outer_update(array_b7, res_mask, full_mask, opm_proj, opm_out))
    pair_loc = pair_stack(pair_loc, pair_mask, pair_mask_t, layer_w[9:])
    value_a7 = lax.all_to_all(array_b7, GROUP_AXIS, 0, 1, tiled=True)
    return value_a7, pair_loc


def solution(mesh):
    row_spec = P((PARTS_AXIS, GROUP_AXIS))

    def local_body(value_a7, pair_loc, value_a12, pair_mask_loc, *weights):
        full_mask = lax.all_gather(value_a12, GROUP_AXIS, axis=0, tiled=True)
        full_pair_mask = lax.all_gather(pair_mask_loc, GROUP_AXIS, axis=0, tiled=True)
        for layer_idx in range(weights[0].shape[0]):
            layer_w = tuple(weight[layer_idx] for weight in weights)
            value_a7, pair_loc = evoformer_block(value_a7, pair_loc, full_mask, full_pair_mask, layer_w)
        return value_a7, pair_loc

    def run_blocks(*arrays):
        n_weights = len(arrays) - 4
        return jax.shard_map(local_body, mesh=mesh, in_specs=(row_spec,) * 4 + (P(),) * n_weights, out_specs=(row_spec, row_spec), check_vma=False)(*arrays)

    return run_blocks
```

profile of v0, /device:TPU:27, one launch (start us, length us, event | category | flops | bytes accessed | tf_op | source)
XLA Modules:
  0.0 1111.0 jit_solution(17521734556548110890)
XLA Ops:
  12.7 14.5 %all_gather.42 = s32[256,128]{1,0:T(8,128)S(1)} all-gather(s32[32,128]{1,0:T(8,128)S(1)} %copy-done.42), channel_id=1, replica_groups=mesh['req'=4,'dap'=8] {'dap'}, dimensions={0}, use_global_device_ids=true | all-gather | bytes 147456 | tf_op jit(solution)/shard_map/all_gather | solution.py:139
  28.0 14.2 %all_gather.43 = bf16[8,128,128]{2,0,1:T(8,128)(2,1)S(1)} all-gather(bf16[8,16,128]{2,0,1:T(8,128)(2,1)S(1)} %fusion.165), channel_id=1, replica_groups=mesh['req'=4,'dap'=8] {'dap'}, dimensions={1}, use_global_device_ids=true | all-gather | bytes 294912 | tf_op jit(solution)/shard_map/all_gather | solution.py:122
  63.7 12.0 %fusion.424 = (f32[32,8,128]{2,1,0:T(8,128)S(1)}, f32[32,8,128,128]{2,3,1,0:T(8,128)}) fusion(f32[8,128,128]{1,2,0:T(8,128)S(1)} %copy.1153, pred[32,128]{1,0:T(8,128)(4,1)S(1)} %dynamic-slice_compare_fusion.1, bf16[32,128,8,32]{1,3,2,0:T(8,128)(2,1)} %bitcast.528, bf16[32,128,8,32]{1,3,2,0:T(8,128)(2,1)} %bitcast.527), kind=kOutput, calls=%fused_computation.597 | convolution fusion | flops 289407104 | bytes 21630976 | tf_op jit(solution)/shard_map/sub | solution.py:37
  75.7 10.7 fusion.26
  86.4 5.6 copy.1155
  104.0 45.9 %all-to-all-done = bf16[32,128,256]{2,0,1:T(8,128)(2,1)} async-done(((bf16[32,128,256]{2,0,1:T(8,128)(2,1)}), bf16[32,128,256]{2,0,1:T(8,128)(2,1)}, u32[]{:S(2)}, u32[]{:S(2)}) %all-to-all-start) | async-done | bytes 2097184 | tf_op jit(solution)/shard_map/all_to_all | solution.py:124
  187.7 20.4 %fusion.425 = (f32[16,8,256]{2,1,0:T(8,128)S(1)}, f32[16,8,256,256]{2,3,1,0:T(8,128)}) fusion(pred[16,256]{1,0:T(8,128)(4,1)S(1)} %compare_bitcast_fusion, bf16[16,256,8,32]{1,3,2,0:T(8,128)(2,1)} %bitcast.535, bf16[16,256,8,32]{1,3,2,0:T(8,128)(2,1)} %bitcast.532), kind=kOutput, calls=%fused_computation.598 | convolution fusion | flops 570425600 | bytes 37883904 | tf_op jit(solution)/shard_map/sub | solution.py:37
  208.0 13.8 %fusion.16 = f32[16,8,32,256]{3,2,1,0:T(8,128)} fusion(bf16[16,256,8,32]{1,3,2,0:T(8,128)(2,1)S(1)} %bitcast.536, f32[16,8,256,256]{2,3,1,0:T(8,128)} %get-tuple-element.41, f32[16,8,256]{2,1,0:T(8,128)S(1)} %get-tuple-element.40), kind=kOutput, calls=%fused_computation.30 | convolution fusion | flops 553648128 | bytes 39976960 | tf_op jit(solution)/shard_map/bhqk,bkhd->bqhd/dot_general | solution.py:38
  221.8 5.5 copy.1172
  227.4 5.6 convert_reduce_fusion.1
  234.3 7.3 convert_reduce_fusion.4
  243.8 14.5 %all_gather.45 = s32[128,128]{1,0:T(8,128)S(1)} all-gather(s32[16,128]{1,0:T(8,128)S(1)} %copy-done.43), channel_id=1, replica_groups=mesh['req'=4,'dap'=8] {'dap'}, dimensions={0}, use_global_device_ids=true | all-gather | bytes 73728 | tf_op jit(solution)/shard_map/all_gather | solution.py:140
  258.4 14.1 %all-gather.7.cloned.1.call-done = bf16[256,128,32]{0,2,1:T(8,128)(2,1)} async-done(((bf16[256,16,32]{0,2,1:T(8,128)(2,1)}), bf16[256,128,32]{0,2,1:T(8,128)(2,1)}) %all-gather.7.cloned.1.call-update) | async-done | bytes 2097168 | tf_op jit(solution)/shard_map/all_gather | solution.py:64
  286.9 45.3 %all-gather.9.cloned.1.call-done = bf16[128,128,128]{2,1,0:T(8,128)(2,1)} async-done(((bf16[16,128,128]{2,1,0:T(8,128)(2,1)}), bf16[128,128,128]{2,1,0:T(8,128)(2,1)}) %all-gather.9.cloned.1.call-update) | async-done | bytes 4194320 | tf_op jit(solution)/shard_map/all_gather | solution.py:96
  332.2 6.7 copy.1195
  355.5 5.7 all-to-all-start.1
  362.4 78.7 %all-to-all-done.1 = bf16[256,16,256]{2,1,0:T(8,128)(2,1)S(1)} async-done(((bf16[256,16,256]{2,1,0:T(8,128)(2,1)}), bf16[256,16,256]{2,1,0:T(8,128)(2,1)S(1)}, u32[]{:S(2)}, u32[]{:S(2)}) %all-to-all-start.1) | async-done | bytes 2097184 | tf_op jit(solution)/shard_map/all_to_all | solution.py:131
  441.2 6.2 all-to-all-start.2
  449.5 10.3 all-to-all-done.2
  462.5 6.7 copy.1209
  475.2 14.4 %all_gather.48 = bf16[4,128,128]{2,0,1:T(4,128)(2,1)S(1)} all-gather(bf16[4,16,128]{2,0,1:T(4,128)(2,1)S(1)} %fusion.167), channel_id=1, replica_groups=mesh['req'=4,'dap'=8] {'dap'}, dimensions={1}, use_global_device_ids=true | all-gather | bytes 147456 | tf_op jit(solution)/shard_map/all_gather | solution.py:88
  505.4 5.9 all-to-all-start.3
  517.6 6.2 all-to-all-done.3
  527.3 14.4 %all_gather.49 = bf16[4,128,128]{2,0,1:T(4,128)(2,1)S(1)} all-gather(bf16[4,16,128]{2,0,1:T(4,128)(2,1)S(1)} %fusion.168), channel_id=1, replica_groups=mesh['req'=4,'dap'=8] {'dap'}, dimensions={1}, use_global_device_ids=true | all-gather | bytes 147456 | tf_op jit(solution)/shard_map/all_gather | solution.py:88
  554.7 5.9 all-to-all-start.4
  587.7 14.9 %all_gather.50 = bf16[8,128,128]{2,0,1:T(8,128)(2,1)S(1)} all-gather(bf16[8,16,128]{2,0,1:T(8,128)(2,1)S(1)} %fusion.166), channel_id=1, replica_groups=mesh['req'=4,'dap'=8] {'dap'}, dimensions={1}, use_global_device_ids=true | all-gather | bytes 294912 | tf_op jit(solution)/shard_map/all_gather | solution.py:122
  602.8 11.7 %fusion.436 = (f32[32,8,128]{2,1,0:T(8,128)S(1)}, f32[32,8,128,128]{2,3,1,0:T(8,128)}) fusion(f32[8,128,128]{1,2,0:T(8,128)S(1)} %copy.1236, pred[32,128]{1,0:T(8,128)(4,1)S(1)} %copy-done.49, bf16[32,128,8,32]{1,3,2,0:T(8,128)(2,1)} %bitcast.525, bf16[32,128,8,32]{1,3,2,0:T(8,128)(2,1)S(1)} %bitcast.522), kind=kOutput, calls=%fused_computation.603 | convolution fusion | flops 289407104 | bytes 21630976 | tf_op jit(solution)/shard_map/sub | solution.py:37
  614.5 10.7 fusion.27
  625.1 5.6 copy.1238
  630.8 5.3 fusion.54
  637.3 51.6 %all_to_all.117 = bf16[32,128,256]{2,0,1:T(8,128)(2,1)S(1)} all-to-all(bf16[32,128,256]{2,0,1:T(8,128)(2,1)S(1)} %copy.1239), channel_id=1, replica_groups=mesh['req'=4,'dap'=8] {'dap'}, dimensions={1} | all-to-all | bytes 4194304 | tf_op jit(solution)/shard_map/all_to_all | solution.py:124
  725.1 20.1 %fusion.437 = (f32[16,8,256]{2,1,0:T(8,128)S(1)}, f32[16,8,256,256]{2,3,1,0:T(8,128)}) fusion(pred[16,256]{1,0:T(8,128)(4,1)S(1)} %copy-done.47, bf16[16,256,8,32]{1,3,2,0:T(8,128)(2,1)} %bitcast.533, bf16[16,256,8,32]{1,3,2,0:T(8,128)(2,1)} %bitcast.531), kind=kOutput, calls=%fused_computation.604 | convolution fusion | flops 570425600 | bytes 37883904 | tf_op jit(solution)/shard_map/sub | solution.py:37
  745.1 13.8 %fusion.17 = f32[16,8,32,256]{3,2,1,0:T(8,128)} fusion(bf16[16,256,8,32]{1,3,2,0:T(8,128)(2,1)S(1)} %bitcast.534, f32[16,8,256,256]{2,3,1,0:T(8,128)} %get-tuple-element.65, f32[16,8,256]{2,1,0:T(8,128)S(1)} %get-tuple-element.64), kind=kOutput, calls=%fused_computation.31 | convolution fusion | flops 553648128 | bytes 39976960 | tf_op jit(solution)/shard_map/bhqk,bkhd->bqhd/dot_general | solution.py:38
  759.0 5.6 copy.1254
  764.6 5.7 convert_reduce_fusion
  771.7 7.1 convert_reduce_fusion.3
  781.5 28.1 %all-gather.13.cloned.1.call-done = bf16[256,128,32]{0,2,1:T(8,128)(2,1)} async-done(((bf16[256,16,32]{0,2,1:T(8,128)(2,1)}), bf16[256,128,32]{0,2,1:T(8,128)(2,1)}) %all-gather.13.cloned.1.call-update) | async-done | bytes 2097168 | tf_op jit(solution)/shard_map/all_gather | solution.py:64
  824.0 45.5 %all-gather.15.cloned.1.call-done = bf16[128,128,128]{2,1,0:T(8,128)(2,1)} async-done(((bf16[16,128,128]{2,1,0:T(8,128)(2,1)}), bf16[128,128,128]{2,1,0:T(8,128)(2,1)}) %all-gather.15.cloned.1.call-update) | async-done | bytes 4194320 | tf_op jit(solution)/shard_map/all_gather | solution.py:96
  869.5 6.7 copy.1273
  890.9 31.7 %all_to_all.118 = bf16[16,128,128]{2,0,1:T(8,128)(2,1)S(1)} all-to-all(bf16[16,128,128]{2,0,1:T(8,128)(2,1)} %copy.1284), channel_id=1, replica_groups=mesh['req'=4,'dap'=8] {'dap'}, dimensions={1} | all-to-all | bytes 1048576 | tf_op jit(solution)/shard_map/all_to_all | solution.py:100
  925.3 19.1 %all-gather.17.cloned.1.call-done = bf16[128,128,128]{2,1,0:T(8,128)(2,1)} async-done(((bf16[16,128,128]{2,1,0:T(8,128)(2,1)}), bf16[128,128,128]{2,1,0:T(8,128)(2,1)}) %all-gather.17.cloned.1.call-update) | async-done | bytes 4194320 | tf_op jit(solution)/shard_map/all_gather | solution.py:101
  944.4 6.7 copy.1287
  959.3 14.3 %all_gather.54 = bf16[4,128,128]{2,0,1:T(4,128)(2,1)S(1)} all-gather(bf16[4,16,128]{2,0,1:T(4,128)(2,1)S(1)} %fusion.169), channel_id=1, replica_groups=mesh['req'=4,'dap'=8] {'dap'}, dimensions={1}, use_global_device_ids=true | all-gather | bytes 147456 | tf_op jit(solution)/shard_map/all_gather | solution.py:88
  987.0 5.8 all-to-all-start.8
  995.9 9.4 all-to-all-done.8
  1006.0 6.3 all-to-all-start.6
  1016.9 49.5 %all_gather.55 = bf16[4,128,128]{2,0,1:T(4,128)(2,1)S(1)} all-gather(bf16[4,16,128]{2,0,1:T(4,128)(2,1)S(1)} %fusion.170), channel_id=1, replica_groups=mesh['req'=4,'dap'=8] {'dap'}, dimensions={1}, use_global_device_ids=true | all-gather | bytes 147456 | tf_op jit(solution)/shard_map/all_gather | solution.py:88
  1089.0 10.9 all-to-all-done.9
  (412 shorter events, 317.9 us)
Async XLA Ops:
  7.2 5.6 copy-start.42
  7.2 20.0 %copy-start.25 = (bf16[16,128,128]{2,1,0:T(8,128)(2,1)S(1)}, bf16[16,128,128]{2,1,0:T(8,128)(2,1)}, u32[]{:S(2)}) copy-start(bf16[16,128,128]{2,1,0:T(8,128)(2,1)} %param.26) | copy-start | bytes 1572868
  7.2 20.6 %copy-start.72 = (bf16[2,128,8]{1,2,0:T(8,128)(2,1)S(1)}, bf16[2,128,8]{1,2,0:T(8,128)(2,1)}, u32[]{:S(2)}) copy-start(bf16[2,128,8]{1,2,0:T(8,128)(2,1)} %param.30) | copy-start | bytes 12292
  7.2 35.2 %copy-start.4 = (bf16[32,128,256]{2,1,0:T(8,128)(2,1)S(1)}, bf16[32,128,256]{2,1,0:T(8,128)(2,1)}, u32[]{:S(2)}) copy-start(bf16[32,128,256]{2,1,0:T(8,128)(2,1)} %param.25) | copy-start | bytes 6291460
  46.4 5.1 copy-start.1
  63.7 12.1 %copy-start.48 = (pred[32,128]{1,0:T(8,128)(4,1)}, pred[32,128]{1,0:T(8,128)(4,1)S(1)}, u32[]{:S(2)}) copy-start(pred[32,128]{1,0:T(8,128)(4,1)S(1)} %dynamic-slice_compare_fusion.1) | copy-start | bytes 12292
  86.4 5.6 copy-start.59
  98.8 51.2 %all-to-all-start = ((bf16[32,128,256]{2,0,1:T(8,128)(2,1)}), bf16[32,128,256]{2,0,1:T(8,128)(2,1)}, u32[]{:S(2)}, u32[]{:S(2)}) async-start(bf16[32,128,256]{2,0,1:T(8,128)(2,1)} %copy.1156), calls=%async_computation | async-start | bytes 4194304 | tf_op jit(solution)/shard_map/all_to_all | solution.py:124
  103.6 168.9 %all-gather.7.cloned.1.call-start = ((), (), s32[]{:S(2)}) async-start(), calls=%async_computation.10 | async-start | bytes 2359296 | tf_op jit(solution)/shard_map/all_gather | solution.py:64
  104.0 168.5 %copy-start.34 = (bf16[256,16]{0,1:T(8,128)(2,1)}, bf16[256,16]{0,1:T(8,128)(2,1)S(1)}, u32[]{:S(2)}) copy-start(bf16[256,16]{0,1:T(8,128)(2,1)S(1)} %convert_element_type.589) | copy-start | bytes 24580
  104.0 83.6 %copy-start.46 = (pred[16,256]{1,0:T(8,128)(4,1)}, pred[16,256]{1,0:T(8,128)(4,1)S(1)}, u32[]{:S(2)}) copy-start(pred[16,256]{1,0:T(8,128)(4,1)S(1)} %compare_bitcast_fusion) | copy-start | bytes 12292
  187.7 20.4 %copy-start.20 = (bf16[16,256,256]{1,2,0:T(8,128)(2,1)S(1)}, bf16[16,256,256]{1,2,0:T(8,128)(2,1)}, u32[]{:S(2)}) copy-start(bf16[16,256,256]{1,2,0:T(8,128)(2,1)} %copy.1167) | copy-start | bytes 6291460
  221.8 5.6 copy-start.61
  234.3 7.9 copy-start.66
  243.7 88.5 %all-gather.9.cloned.1.call-start = ((), (), s32[]{:S(2)}) async-start(), calls=%async_computation.11 | async-start | bytes 4718592 | tf_op jit(solution)/shard_map/all_gather | solution.py:96
  258.2 88.5 %copy-start.36 = (f32[16,128]{1,0:T(8,128)}, f32[16,128]{1,0:T(8,128)S(1)}, u32[]{:S(2)}) copy-start(f32[16,128]{1,0:T(8,128)S(1)} %dynamic-slice_convert_fusion) | copy-start | bytes 24580
  258.4 21.7 %copy-start.44 = (f32[16,128]{1,0:T(8,128)}, f32[16,128]{1,0:T(8,128)S(1)}, u32[]{:S(2)}) copy-start(f32[16,128]{1,0:T(8,128)S(1)} %convolution_add_fusion) | copy-start | bytes 24580
  286.5 176.0 %all-gather.11.cloned.1.call-start = ((), (), s32[]{:S(2)}) async-start(), calls=%async_computation.12 | async-start | bytes 4718592 | tf_op jit(solution)/shard_map/all_gather | solution.py:101
  338.9 4.9 copy-start.15
  338.9 4.9 copy-start.68
  355.5 85.7 %all-to-all-start.1 = ((bf16[256,16,256]{2,1,0:T(8,128)(2,1)}), bf16[256,16,256]{2,1,0:T(8,128)(2,1)S(1)}, u32[]{:S(2)}, u32[]{:S(2)}) async-start(bf16[256,16,256]{2,1,0:T(8,128)(2,1)} %copy.1177), calls=%async_computation.1 | async-start | bytes 4194304 | tf_op jit(solution)/shard_map/all_to_all | solution.py:131
  441.2 18.6 %all-to-all-start.2 = ((bf16[16,128,128]{2,0,1:T(8,128)(2,1)}), bf16[16,128,128]{2,0,1:T(8,128)(2,1)S(1)}, u32[]{:S(2)}, u32[]{:S(2)}) async-start(bf16[16,128,128]{2,0,1:T(8,128)(2,1)} %copy.1206), calls=%async_computation.2 | async-start | bytes 1048576 | tf_op jit(solution)/shard_map/all_to_all | solution.py:100
  447.5 97.3 %copy-start.52 = (pred[16,128]{1,0:T(8,128)(4,1)}, pred[16,128]{1,0:T(8,128)(4,1)S(1)}, u32[]{:S(2)}) copy-start(pred[16,128]{1,0:T(8,128)(4,1)S(1)} %copy.1225) | copy-start | bytes 6148
  447.6 47.0 %copy-start.54 = (pred[16,128]{1,0:T(8,128)(4,1)}, pred[16,128]{1,0:T(8,128)(4,1)S(1)}, u32[]{:S(2)}) copy-start(pred[16,128]{1,0:T(8,128)(4,1)S(1)} %dynamic-slice_compare_fusion.2) | copy-start | bytes 6148
  505.4 18.4 %all-to-all-start.3 = ((bf16[16,128,128]{2,0,1:T(8,128)(2,1)}), bf16[16,128,128]{2,0,1:T(8,128)(2,1)S(1)}, u32[]{:S(2)}, u32[]{:S(2)}) async-start(bf16[16,128,128]{2,0,1:T(8,128)(2,1)} %copy.1221), calls=%async_computation.3 | async-start | bytes 1048576 | tf_op jit(solution)/shard_map/all_to_all | solution.py:105
  517.6 9.5 copy-start.50
  553.2 7.7 copy-start.11
  554.7 25.1 %all-to-all-start.4 = ((bf16[128,16,128]{2,1,0:T(8,128)(2,1)}), bf16[128,16,128]{2,1,0:T(8,128)(2,1)S(1)}, u32[]{:S(2)}, u32[]{:S(2)}) async-start(bf16[128,16,128]{2,1,0:T(8,128)(2,1)} %copy.1230), calls=%async_computation.4 | async-start | bytes 1048576 | tf_op jit(solution)/shard_map/all_to_all | solution.py:108
  560.6 248.9 %all-gather.13.cloned.1.call-start = ((), (), s32[]{:S(2)}) async-start(), calls=%async_computation.13 | async-start | bytes 2359296 | tf_op jit(solution)/shard_map/all_gather | solution.py:64
  582.4 5.0 copy-start.73
  582.5 20.3 %copy-start.16 = (bf16[32,128,256]{1,2,0:T(8,128)(2,1)S(1)}, bf16[32,128,256]{1,2,0:T(8,128)(2,1)}, u32[]{:S(2)}) copy-start(bf16[32,128,256]{1,2,0:T(8,128)(2,1)} %copy.1182) | copy-start | bytes 6291460
  582.5 20.3 %copy-start.49 = (pred[32,128]{1,0:T(8,128)(4,1)S(1)}, pred[32,128]{1,0:T(8,128)(4,1)}, u32[]{:S(2)}) copy-start(pred[32,128]{1,0:T(8,128)(4,1)} %copy-done.48) | copy-start | bytes 12292
  625.1 5.6 copy-start.60
  718.8 6.3 copy-start.47
  725.1 20.1 %copy-start.19 = (bf16[16,256,256]{1,2,0:T(8,128)(2,1)S(1)}, bf16[16,256,256]{1,2,0:T(8,128)(2,1)}, u32[]{:S(2)}) copy-start(bf16[16,256,256]{1,2,0:T(8,128)(2,1)} %copy.1250) | copy-start | bytes 6291460
  759.0 5.6 copy-start.62
  764.6 7.1 copy-start.56
  771.7 7.8 copy-start.67
  780.9 88.6 %all-gather.15.cloned.1.call-start = ((), (), s32[]{:S(2)}) async-start(), calls=%async_computation.14 | async-start | bytes 4718592 | tf_op jit(solution)/shard_map/all_gather | solution.py:96
  823.8 52.4 %copy-start.22 = (bf16[16,128,128]{1,2,0:T(8,128)(2,1)S(1)}, bf16[16,128,128]{1,2,0:T(8,128)(2,1)}, u32[]{:S(2)}) copy-start(bf16[16,128,128]{1,2,0:T(8,128)(2,1)} %get-tuple-element.16) | copy-start | bytes 1572868
  823.8 120.6 %all-gather.17.cloned.1.call-start = ((), (), s32[]{:S(2)}) async-start(), calls=%async_computation.15 | async-start | bytes 4718592 | tf_op jit(solution)/shard_map/all_gather | solution.py:101
  956.7 19.5 %copy-start.55 = (pred[16,128]{1,0:T(8,128)(4,1)S(1)}, pred[16,128]{1,0:T(8,128)(4,1)}, u32[]{:S(2)}) copy-start(pred[16,128]{1,0:T(8,128)(4,1)} %copy-done.54) | copy-start | bytes 6148
  987.0 18.2 %all-to-all-start.8 = ((bf16[16,128,128]{2,0,1:T(8,128)(2,1)}), bf16[16,128,128]{2,0,1:T(8,128)(2,1)S(1)}, u32[]{:S(2)}, u32[]{:S(2)}) async-start(bf16[16,128,128]{2,0,1:T(8,128)(2,1)} %copy.1299), calls=%async_computation.8 | async-start | bytes 1048576 | tf_op jit(solution)/shard_map/all_to_all | solution.py:105
  1006.0 76.6 %all-to-all-start.6 = ((bf16[256,16,256]{2,1,0:T(8,128)(2,1)}), bf16[256,16,256]{2,1,0:T(8,128)(2,1)S(1)}, u32[]{:S(2)}, u32[]{:S(2)}) async-start(bf16[256,16,256]{2,1,0:T(8,128)(2,1)} %copy.1259), calls=%async_computation.6 | async-start | bytes 4194304 | tf_op jit(solution)/shard_map/all_to_all | solution.py:131
  1015.2 56.4 %copy-start.53 = (pred[16,128]{1,0:T(8,128)(4,1)S(1)}, pred[16,128]{1,0:T(8,128)(4,1)}, u32[]{:S(2)}) copy-start(pred[16,128]{1,0:T(8,128)(4,1)} %copy-done.52) | copy-start | bytes 6148
  1082.6 17.3 %all-to-all-start.9 = ((bf16[128,16,128]{2,1,0:T(8,128)(2,1)}), bf16[128,16,128]{2,1,0:T(8,128)(2,1)S(1)}, u32[]{:S(2)}, u32[]{:S(2)}) async-start(bf16[128,16,128]{2,1,0:T(8,128)(2,1)} %copy.1307), calls=%async_computation.9 | async-start | bytes 1048576 | tf_op jit(solution)/shard_map/all_to_all | solution.py:108
  1089.0 12.8 %copy-start.64 = (bf16[2,512,128]{2,1,0:T(8,128)(2,1)S(1)}, bf16[2,512,128]{2,1,0:T(8,128)(2,1)}, u32[]{:S(2)}) copy-start(bf16[2,512,128]{2,1,0:T(8,128)(2,1)} %param.49) | copy-start | bytes 786436
  1089.0 12.8 %copy-start.65 = (bf16[2,128,512]{2,1,0:T(8,128)(2,1)S(1)}, bf16[2,128,512]{2,1,0:T(8,128)(2,1)}, u32[]{:S(2)}) copy-start(bf16[2,128,512]{2,1,0:T(8,128)(2,1)} %param.48) | copy-start | bytes 786436
  (42 other events, 109.9 us)
Sparse Core Ops, SparseCore 0:
  243.8 28.6 all-gather.6
  286.6 45.5 all-gather.8
  352.5 84.5 all-gather.10
  781.1 28.4 all-gather.12
  823.9 45.5 all-gather.14
  889.8 54.5 all-gather.16
where the time goes:
time: 1120 us; the launch traced here: 1110 us
  waiting for transfers between devices  313 us (28%)
  matrix products  247 us (22%)
  blocking collectives  234 us (21%)
  local copies, waits for them, and re-layouts  203 us (18%)
  other arithmetic  49.9 us (4%)
  starting transfers between devices  47.4 us (4%)
  between operations  16.2 us (1%)
    all_gather x4, waiting for transfers between devices, pair_stack(): right_full = lax.all_gather(right_act, GROUP_AXIS, axis=0, tiled=True)  110 us
    all_gather x4, blocking collectives, tri_attention(): lax.all_gather(head_bias(pair_norm, w_bias), GROUP_AXIS, axis=1, tiled=True)  92.6 us
    sub x8, matrix products, attend(): attn_prob = jax.nn.softmax(logits, axis=-1).astype(jnp.bfloat16)  84 us
    all_to_all x2, waiting for transfers between devices, evoformer_block(): value_a7 = lax.all_to_all(array_b7, GROUP_AXIS, 0, 1, tiled=True)  78.7 us
    dot_general x32, matrix products, dense(): jnp.einsum('...c,cf->...f', x, weight, preferred_element_type=jnp.float32)  75.3 us
    dot_general x8, matrix products, attend(): jnp.einsum('bhqk,bkhd->bqhd', attn_prob, v_heads, preferred_element_type=...  60.9 us
    all_to_all x1, blocking collectives, evoformer_block(): array_b7 = lax.all_to_all(value_a7, GROUP_AXIS, 1, 0, tiled=True)  51.6 us
    all_to_all x1, waiting for transfers between devices, evoformer_block(): array_b7 = lax.all_to_all(value_a7, GROUP_AXIS, 1, 0, tiled=True)  45.9 us
  transfers between devices with their start and end apart: 14, of which 11 were waited for; matrix products, arithmetic and copies ran while one was open for 5% of the time, Pallas kernels for 0%

commit v1 on v0

v1 whole, which is shorter than its diff:
```python
import functools

import jax
import jax.numpy as jnp
from jax import lax
from jax.experimental import pallas as pl
from jax.experimental.pallas import tpu as pltpu
from jax.sharding import PartitionSpec as P

MESH = pl.DeviceIdType.MESH
F32 = jnp.float32
BF = jnp.bfloat16
LOG2E = 1.4426950408889634
NEG = -1e9 * LOG2E
ND = 8
VMEM_LIMIT = 66_000_000
RB = 128
SQ = 256
TI = 16
HD = 32


def dot(a, b):
    return lax.dot_general(a, b, (((1,), (0,)), ((), ())), preferred_element_type=F32)


def dot_nt(a, b):
    return lax.dot_general(a, b, (((1,), (1,)), ((), ())), preferred_element_type=F32)


def dot_tn(a, b):
    return lax.dot_general(a, b, (((0,), (0,)), ((), ())), preferred_element_type=F32)


def transpose_bf(w):
    return w.astype(F32).T.astype(BF)


def norm_lanes(x):
    mean = jnp.mean(x, axis=-1, keepdims=True)
    centered = x - mean
    var = jnp.mean(centered * centered, axis=-1, keepdims=True)
    return (centered * lax.rsqrt(var + 1e-5)).astype(BF)


def norm_rows(x):
    mean = jnp.mean(x, axis=0, keepdims=True)
    centered = x - mean
    var = jnp.mean(centered * centered, axis=0, keepdims=True)
    return (centered * lax.rsqrt(var + 1e-5)).astype(BF)


def residual(x, update):
    return (x.astype(F32) + update).astype(BF)


def group_barrier(me):
    sem = pltpu.get_barrier_semaphore()
    for p in range(1, ND):
        pl.semaphore_signal(sem, inc=1, device_id={'dap': lax.rem(me + p, ND)}, device_id_type=MESH)
    pl.semaphore_wait(sem, ND - 1)


def remote(src, dst, send_sem, recv_sem, peer):
    return pltpu.make_async_remote_copy(src_ref=src, dst_ref=dst, send_sem=send_sem, recv_sem=recv_sem,
                                        device_id={'dap': peer}, device_id_type=MESH)


class Direct:
    def __init__(self, me, src_of, dst_of, ssem, rsem, base=0):
        self.me, self.src_of, self.dst_of, self.ssem, self.rsem, self.base = me, src_of, dst_of, ssem, rsem, base

    def copy_to(self, p):
        peer = lax.rem(self.me + p, ND)
        return remote(self.src_of(peer), self.dst_of(self.me), self.ssem.at[self.base + p], self.rsem.at[self.base + p], peer)

    def start(self, ps=range(1, ND)):
        for p in ps:
            self.copy_to(p).start()

    def wait_recv(self):
        for p in range(1, ND):
            owner = lax.rem(self.me + ND - p, ND)
            remote(self.src_of(owner), self.dst_of(owner), self.ssem.at[self.base + p], self.rsem.at[self.base + p], owner).wait_recv()

    def wait_send(self):
        for p in range(1, ND):
            self.copy_to(p).wait_send()


class Chain:
    def __init__(self, me, buf, ssem, rsem):
        self.buf, self.ssem, self.rsem = buf, ssem, rsem
        self.z, self.c = lax.div(me, 2), lax.rem(me, 2)
        self.me, self.partner = me, me + 1 - 2 * self.c

    def cp(self, slot, peer, sem):
        return remote(self.buf.at[slot], self.buf.at[slot], self.ssem.at[sem], self.rsem.at[sem], peer)

    def slot(self, off, other=False):
        core = 1 - self.c if other else self.c
        return (self.z + off) * 2 + core

    def start(self):
        @pl.when(self.z < 3)
        def _():
            self.cp(self.me, self.me + 2, 0).start()

        @pl.when(self.z > 0)
        def _():
            self.cp(self.me, self.me - 2, 3).start()

        self.cp(self.me, self.partner, 6).start()

    def finish(self):
        z = self.z
        for t in range(1, 4):
            @pl.when(z >= t)
            def _():
                self.cp(self.slot(-t), self.me, t - 1).wait_recv()
                if t < 3:
                    @pl.when(z < 3)
                    def _():
                        self.cp(self.slot(-t), self.me + 2, t).start()
                self.cp(self.slot(-t), self.partner, 6 + t).start()

            @pl.when(z + t <= 3)
            def _():
                self.cp(self.slot(t), self.me, 3 + t - 1).wait_recv()
                if t < 3:
                    @pl.when(z > 0)
                    def _():
                        self.cp(self.slot(t), self.me - 2, 3 + t).start()
                self.cp(self.slot(t), self.partner, 9 + t).start()
        self.cp(self.partner, self.me, 6).wait_recv()
        for t in range(1, 4):
            @pl.when(z >= t)
            def _():
                self.cp(self.slot(-t, True), self.me, 6 + t).wait_recv()

            @pl.when(z + t <= 3)
            def _():
                self.cp(self.slot(t, True), self.me, 9 + t).wait_recv()

    def wait_send(self):
        z = self.z

        @pl.when(z < 3)
        def _():
            self.cp(self.me, self.me + 2, 0).wait_send()

        @pl.when(z > 0)
        def _():
            self.cp(self.me, self.me - 2, 3).wait_send()

        self.cp(self.me, self.partner, 6).wait_send()
        for t in range(1, 4):
            @pl.when(z >= t)
            def _():
                if t < 3:
                    @pl.when(z < 3)
                    def _():
                        self.cp(self.slot(-t), self.me + 2, t).wait_send()
                self.cp(self.slot(-t), self.partner, 6 + t).wait_send()

            @pl.when(z + t <= 3)
            def _():
                if t < 3:
                    @pl.when(z > 0)
                    def _():
                        self.cp(self.slot(t), self.me - 2, 3 + t).wait_send()
                self.cp(self.slot(t), self.partner, 9 + t).wait_send()


def column_of(row):
    return jnp.broadcast_to(row, (RB, row.shape[1])).T


def attend_tile(xn, wt_ref, wk, w_out, heads, bias_ref, key_mask):
    length = xn.shape[0]
    width = heads * HD
    proj = dot_nt(wt_ref[...], xn)
    q_t = proj[:width].astype(BF)
    v_t = proj[width:2 * width].astype(BF)
    gate = jax.nn.sigmoid(proj[2 * width:].astype(BF).astype(F32))
    keys = dot(xn, wk).astype(BF)
    valid = key_mask > 0
    scale = HD ** -0.5 * LOG2E
    pieces = []
    for qc in range(length // RB):
        outs = []
        for h in range(heads):
            hh = h % 4
            q_h = q_t[HD * h:HD * h + HD, RB * qc:RB * qc + RB]
            rhs = [q_h]
            if hh > 0:
                rhs = [jnp.zeros((HD * hh, RB), BF)] + rhs
            if hh < 3:
                rhs = rhs + [jnp.zeros((96 - HD * hh, RB), BF)]
            logits = dot(keys[:, RB * (h // 4):RB * (h // 4) + RB], jnp.concatenate(rhs, 0)) * scale
            if bias_ref is not None:
                logits = logits + bias_ref[h]
            logits = jnp.where(valid, logits, NEG)
            top = jnp.max(logits, axis=0, keepdims=True)
            e = jnp.exp2(logits - top)
            inv = 1.0 / jnp.sum(e, axis=0, keepdims=True)
            prob = (e * inv).astype(BF)
            outs.append(dot(v_t[HD * h:HD * h + HD], prob))
        gated = (jnp.concatenate(outs, 0) * gate[:, RB * qc:RB * qc + RB]).astype(BF)
        pieces.append(dot_tn(gated, w_out))
    return pieces


def prep_qkvg(w_ref, wt_ref, width):
    wt_ref[0:width, :] = transpose_bf(w_ref[0, :, 0:width])
    wt_ref[width:3 * width, :] = transpose_bf(w_ref[0, :, 2 * width:4 * width])


def mask_kernel(mm_ref, pm_ref, mt_ref, pt_ref, mbuf, pbuf, ssem, rsem):
    me = lax.axis_index('dap')
    group_barrier(me)
    mbuf[me] = mm_ref[...].astype(F32)
    pbuf[me] = pm_ref[...].astype(F32)
    ex_m = Direct(me, lambda peer: mbuf.at[me], lambda owner: mbuf.at[owner], ssem, rsem, 0)
    ex_p = Direct(me, lambda peer: pbuf.at[me], lambda owner: pbuf.at[owner], ssem, rsem, ND)
    ex_m.start()
    ex_p.start()
    ex_m.wait_recv()
    ex_p.wait_recv()
    mt_ref[...] = mbuf[...].reshape(SQ, RB).T
    pt_ref[...] = pbuf[...].reshape(RB, RB).T
    ex_m.wait_send()
    ex_p.wait_send()


def msa_kernel(m_ref, z_ref, rmask_ref, mt_ref, row_w, row_b, row_o, col_w, col_o, mtr_i, mtr_o, opm_p,
               m2_ref, at_ref, bt_ref,
               bloc, ball, bias_t, wt, opt, scr, sendbuf, rbuf, bscr, ssem, rsem):
    me = lax.axis_index('dap')
    group_barrier(me)
    wb = jnp.concatenate([row_b[0], jnp.zeros((RB, 120), BF)], 1)
    wb_t = transpose_bf(wb)[0:8]

    def bias_row(i, carry):
        xn = norm_lanes(z_ref[i].astype(F32))
        bscr[pl.ds(i, 8, stride=TI), :] = dot_nt(wb_t, xn)
        return carry

    lax.fori_loop(0, TI, bias_row, 0)
    ball[me] = bscr[...].astype(BF).reshape(8, TI, RB)
    ex_b = Direct(me, lambda peer: ball.at[me], lambda owner: ball.at[owner], ssem, rsem, 0)
    ex_b.start()
    prep_qkvg(row_w, wt, SQ)
    opt[...] = transpose_bf(jnp.concatenate([opm_p[0], jnp.zeros((SQ, 64), BF)], 1))[0:64]
    ex_b.wait_recv()
    for h in range(8):
        bias_t[h] = ball[:, h].reshape(RB, RB).astype(F32).T * LOG2E
    row_k = row_w[0, :, SQ:512]
    row_ow = row_o[0]
    exchanges = []
    for ck in range(2):
        def row_body(sl, carry):
            s = ck * TI + sl
            x = m_ref[s]
            key_mask = column_of(rmask_ref[pl.ds(s, 1), :])
            upd, = attend_tile(norm_lanes(x.astype(F32)), wt, row_k, row_ow, 8, bias_t, key_mask)
            y = residual(x, upd).astype(F32)
            for half in range(2):
                scr[half, pl.ds(sl, RB, stride=TI), :] = y[:, RB * half:RB * half + RB]
            return carry

        lax.fori_loop(0, TI, row_body, 0)

        def pack(d, carry):
            for half in range(2):
                part = scr[half, pl.ds(pl.multiple_of(d * SQ, SQ), SQ), :].astype(BF).reshape(TI, TI, RB)
                sendbuf[ck, d, :, :, RB * half:RB * half + RB] = part
            return carry

        lax.fori_loop(0, 8, pack, 0)
        ex = Direct(me, lambda peer: sendbuf.at[ck, peer], lambda owner: rbuf.at[owner * 2 + ck], ssem, rsem, 8 * (ck + 1))
        ex.start()
        exchanges.append(ex)
        rbuf[me * 2 + ck] = sendbuf[ck, me]
    ex_b.wait_send()
    prep_qkvg(col_w, wt, SQ)
    for ex in exchanges:
        ex.wait_recv()
    col_k = col_w[0, :, SQ:512]
    col_ow = col_o[0]

    def col_body(r, carry):
        x = rbuf[:, r].reshape(SQ, SQ)
        mrow = mt_ref[pl.ds(me * TI + r, 1), :]
        key_mask = column_of(mrow)
        upd = attend_tile(norm_lanes(x.astype(F32)), wt, col_k, col_ow, 8, None, key_mask)
        y = residual(x, jnp.concatenate(upd, 0))
        hid = jnp.maximum(dot(norm_lanes(y.astype(F32)), mtr_i[0]), 0.0).astype(BF)
        y2 = residual(y, dot(hid, mtr_o[0]))
        m2_ref[r] = y2
        ab = dot_nt(opt[...], norm_lanes(y2.astype(F32))).astype(BF).astype(F32) * mrow
        at_ref[r] = ab[0:HD].astype(BF)
        for half in range(2):
            scr[half, pl.ds(r, HD, stride=TI), :] = ab[HD:64, RB * half:RB * half + RB]
        return carry

    lax.fori_loop(0, TI, col_body, 0)
    for half in range(2):
        bt_ref[:, :, RB * half:RB * half + RB] = scr[half, 0:512, :].astype(BF).reshape(HD, TI, RB)
    for ex in exchanges:
        ex.wait_send()


def pair_kernel(m2_ref, at_ref, bt_ref, z_ref, mt_ref, pm_ref, pt_ref,
                opm_o, tmo_p, tmo_o, tmi_p, tmi_o, tas_w, tas_b, tas_o, tae_w, tae_b, tae_o, ptr_i, ptr_o,
                mout_ref, zout_ref,
                btall, obuf, opw, scr_a, scr_b, scr_x, a_c, ball1, ball2, gbuf, z1, zcol, sbias, ball3, bias_t,
                wt, twt, zsend, z4, mrecv, mscr,
                ch_s, ch_r, ds, dr):
    me = lax.axis_index('dap')
    group_barrier(me)
    btall[me] = bt_ref[...]
    ag0 = Chain(me, btall, ch_s.at[0], ch_r.at[0])
    ag0.start()
    scr_a[0:1024, :] = opm_o[0].astype(F32)

    def perm(e, carry):
        rows = scr_a[pl.ds(e, HD, stride=HD), :]
        scr_b[pl.ds(pl.multiple_of(e * HD, HD), HD), :] = rows
        return carry

    lax.fori_loop(0, HD, perm, 0)
    for q in range(8):
        opw[:, RB * q:RB * q + RB] = scr_b[RB * q:RB * q + RB, :].T.astype(BF)
    mloc = mt_ref[pl.ds(pl.multiple_of(me * TI, TI), TI), :].astype(BF)
    inv_over = 1.0 / (1e-3 + dot_nt(mloc, mt_ref[...].astype(BF)))
    scr_x[0:TI, :] = inv_over
    ag0.finish()

    left = at_ref[...].reshape(512, SQ)

    def opm_e(e, carry):
        rhs = btall[:, e].reshape(RB, SQ)
        o = dot_nt(left, rhs).astype(BF).reshape(TI, HD, RB)
        obuf[:, pl.ds(pl.multiple_of(e * HD, HD), HD), :] = o
        return carry

    lax.fori_loop(0, HD, opm_e, 0)

    ex_m = Direct(me, lambda peer: m2_ref.at[:, pl.ds(pl.multiple_of(peer * HD, HD), HD), :], lambda owner: mrecv.at[owner], ds, dr, 0)
    mrecv[me] = m2_ref[:, pl.ds(pl.multiple_of(me * HD, HD), HD), :]
    ex_m.start([1, 2])

    def opm_i(i, carry):
        y_t = dot(opw[...], obuf[i]) * scr_x[pl.ds(i, 1), :]
        z1[i] = residual(z_ref[i], y_t.T)
        return carry

    lax.fori_loop(0, TI, opm_i, 0)

    def front(w_ref, z_src, ball, left_too):
        wt_l = twt
        wt_l[...] = transpose_bf(w_ref[0, :, 0:512])
        wg = w_ref[0, :, 512:640]

        def body(i, carry):
            xn = norm_lanes(z_src[i].astype(F32))
            mrow = pm_ref[pl.ds(i, 1), :]
            if left_too:
                pr = dot_nt(wt_l[...], xn)
                scr_a[pl.ds(i, RB, stride=TI), :] = mrow * jax.nn.sigmoid(pr[SQ:384]) * pr[0:RB]
                pb, pg = pr[RB:SQ], pr[384:512]
            else:
                pb = dot_nt(wt_l[RB:SQ, :], xn)
                pg = dot_nt(wt_l[384:512, :], xn)
            scr_b[pl.ds(i, RB, stride=TI), :] = mrow * jax.nn.sigmoid(pg) * pb
            gbuf[i] = jax.nn.sigmoid(dot(xn, wg))
            return carry

        lax.fori_loop(0, TI, body, 0)
        ball[me] = scr_b[...].astype(BF).reshape(RB, TI, RB)

    def finish(w_ref, z_src, z_dst):
        w = w_ref[0]

        def body(i, carry):
            xn = norm_rows(scr_x[pl.ds(i, RB, stride=TI), :])
            z_dst[i] = residual(z_src[i], gbuf[i] * dot_tn(xn, w))
            return carry

        lax.fori_loop(0, TI, body, 0)

    front(tmo_p, z1, ball1, True)
    ag1 = Chain(me, ball1, ch_s.at[1], ch_r.at[1])
    ag1.start()
    a_c[...] = scr_a[...].astype(BF).reshape(RB, TI, RB)
    ag1.finish()

    def out_c(cc, carry):
        for u in range(8):
            c = cc * 8 + u
            scr_x[pl.ds(pl.multiple_of(c * TI, TI), TI), :] = dot_nt(a_c[c], ball1[:, c].reshape(RB, RB))
        return carry

    lax.fori_loop(0, TI, out_c, 0)
    ex_m.start([3, 4])
    finish(tmo_o, z1, z1)

    ex_z1 = Direct(me, lambda peer: z1.at[:, pl.ds(pl.multiple_of(peer * TI, TI), TI), :], lambda owner: zcol.at[0, owner], ds, dr, 8)
    ex_z1.start()
    zcol[0, me] = z1[:, pl.ds(pl.multiple_of(me * TI, TI), TI), :]
    front(tmi_p, z1, ball2, False)
    ag2 = Chain(me, ball2, ch_s.at[2], ch_r.at[2])
    ag2.start()
    ex_z1.wait_recv()
    scr_b[...] = zcol[0].astype(F32).reshape(2048, RB)

    def in_left(i, carry):
        xn = norm_lanes(scr_b[pl.ds(i, RB, stride=TI), :])
        mrow = pt_ref[pl.ds(me * TI + i, 1), :]
        pa = dot_nt(twt[0:RB, :], xn)
        pg = dot_nt(twt[SQ:384, :], xn)
        scr_a[pl.ds(i, RB, stride=TI), :] = mrow * jax.nn.sigmoid(pg) * pa
        return carry

    lax.fori_loop(0, TI, in_left, 0)
    a_c[...] = scr_a[...].astype(BF).reshape(RB, TI, RB)
    ag2.finish()

    def in_c(cc, carry):
        for u in range(8):
            c = cc * 8 + u
            scr_x[pl.ds(pl.multiple_of(c * TI, TI), TI), :] = dot(a_c[c], ball2[:, c].reshape(RB, RB))
        return carry

    lax.fori_loop(0, TI, in_c, 0)
    ex_z1.wait_send()
    ex_m.start([5, 6, 7])
    finish(tmi_o, z1, z1)

    def tri_bias(w_ref, tile, slot, base):
        wb_t = transpose_bf(jnp.concatenate([w_ref[0], jnp.zeros((RB, 124), BF)], 1))[0:8]

        def body(i, carry):
            sbias[pl.ds(i, 8, stride=TI), :] = dot_nt(wb_t, norm_lanes(tile(i)))
            return carry

        lax.fori_loop(0, TI, body, 0)
        ball3[slot, me] = sbias[0:64, :].astype(BF).reshape(4, TI, RB)
        ex = Direct(me, lambda peer: ball3.at[slot, me], lambda owner: ball3.at[slot, owner], ds, dr, base)
        ex.start()
        return ex

    def take_bias(slot):
        for h in range(4):
            bias_t[h] = ball3[slot, :, h].reshape(RB, RB).astype(F32).T * LOG2E

    ex_s = tri_bias(tas_b, lambda i: z1[i].astype(F32), 0, TI)
    prep_qkvg(tas_w, wt, RB)
    ex_s.wait_recv()
    take_bias(0)
    tas_k = tas_w[0, :, RB:SQ]

    def tas_body(i, carry):
        x = z1[i]
        upd, = attend_tile(norm_lanes(x.astype(F32)), wt, tas_k, tas_o[0], 4, bias_t, column_of(pm_ref[pl.ds(i, 1), :]))
        z1[i] = residual(x, upd)
        return carry

    lax.fori_loop(0, TI, tas_body, 0)

    ex_z2 = Direct(me, lambda peer: z1.at[:, pl.ds(pl.multiple_of(peer * TI, TI), TI), :], lambda owner: zcol.at[1, owner], ds, dr, 24)
    ex_z2.start()
    zcol[1, me] = z1[:, pl.ds(pl.multiple_of(me * TI, TI), TI), :]
    prep_qkvg(tae_w, wt, RB)
    ex_z2.wait_recv()
    scr_b[...] = zcol[1].astype(F32).reshape(2048, RB)
    ex_e = tri_bias(tae_b, lambda i: scr_b[pl.ds(i, RB, stride=TI), :], 1, HD)
    ex_e.wait_recv()
    take_bias(1)
    tae_k = tae_w[0, :, RB:SQ]

    def tae_body(i, carry):
        x = scr_b[pl.ds(i, RB, stride=TI), :]
        upd, = attend_tile(norm_lanes(x), wt, tae_k, tae_o[0], 4, bias_t, column_of(pt_ref[pl.ds(me * TI + i, 1), :]))
        scr_a[pl.ds(i, RB, stride=TI), :] = x + upd
        return carry

    lax.fori_loop(0, TI, tae_body, 0)
    zsend[...] = scr_a[...].astype(BF).reshape(8, TI, TI, RB)
    ex_z3 = Direct(me, lambda peer: zsend.at[peer], lambda owner: z4.at[:, pl.ds(pl.multiple_of(owner * TI, TI), TI), :], ds, dr, 40)
    ex_z3.start()
    z4[:, pl.ds(pl.multiple_of(me * TI, TI), TI), :] = zsend[me]

    ex_m.wait_recv()

    def widen(d, carry):
        for half in range(2):
            part = mrecv[d, :, :, RB * half:RB * half + RB].astype(F32).reshape(512, RB)
            mscr[half, pl.ds(pl.multiple_of(d * 512, 512), 512), :] = part
        return carry

    lax.fori_loop(0, 8, widen, 0)

    def take_seq(s, carry):
        for half in range(2):
            mout_ref[s, :, RB * half:RB * half + RB] = mscr[half, pl.ds(s, RB, stride=HD), :].astype(BF)
        return carry

    lax.fori_loop(0, HD, take_seq, 0)
    ex_z3.wait_recv()

    def trans(i, carry):
        x = z4[i]
        hid = jnp.maximum(dot(norm_lanes(x.astype(F32)), ptr_i[0]), 0.0).astype(BF)
        zout_ref[i] = residual(x, dot(hid, ptr_o[0]))
        return carry

    lax.fori_loop(0, TI, trans, 0)
    for ex in (ag0, ag1, ag2, ex_m, ex_s, ex_e, ex_z2, ex_z3):
        ex.wait_send()


def full(shape):
    return pl.BlockSpec(shape, lambda g: (0,) * len(shape))


def layer_of(shape, layer):
    return pl.BlockSpec((1,) + shape[1:], lambda g: (layer,) + (0,) * (len(shape) - 1))


def params(cid):
    return pltpu.CompilerParams(collective_id=cid, has_side_effects=True, vmem_limit_bytes=VMEM_LIMIT)


def run_masks(mm, pm):
    outs = [(RB, SQ), (RB, RB)]
    return pl.pallas_call(
        mask_kernel,
        grid=(1,),
        out_shape=[jax.ShapeDtypeStruct(s, F32) for s in outs],
        in_specs=[full(mm.shape), full(pm.shape)],
        out_specs=[full(s) for s in outs],
        scratch_shapes=[pltpu.VMEM((ND, HD, RB), F32), pltpu.VMEM((ND, TI, RB), F32),
                        pltpu.SemaphoreType.DMA((TI,)), pltpu.SemaphoreType.DMA((TI,))],
        compiler_params=params(0),
    )(mm, pm)


def run_msa(layer, m, z, rmask, mt, weights):
    acts = (m, z, rmask, mt)
    outs = [(TI, SQ, SQ), (TI, HD, SQ), (HD, TI, SQ)]
    return pl.pallas_call(
        msa_kernel,
        grid=(1,),
        out_shape=[jax.ShapeDtypeStruct(s, BF) for s in outs],
        in_specs=[full(a.shape) for a in acts] + [layer_of(w.shape, layer) for w in weights],
        out_specs=[full(s) for s in outs],
        scratch_shapes=[
            pltpu.VMEM((8, TI, RB), BF),
            pltpu.VMEM((ND, 8, TI, RB), BF),
            pltpu.VMEM((8, RB, RB), F32),
            pltpu.VMEM((768, SQ), BF),
            pltpu.VMEM((64, SQ), BF),
            pltpu.VMEM((2, 2048, RB), F32),
            pltpu.VMEM((2, ND, TI, TI, SQ), BF),
            pltpu.VMEM((2 * ND, TI, TI, SQ), BF),
            pltpu.VMEM((RB, RB), F32),
            pltpu.SemaphoreType.DMA((24,)), pltpu.SemaphoreType.DMA((24,)),
        ],
        compiler_params=params(1 + 2 * layer),
    )(*acts, *weights)


def run_pair(layer, m2, at, bt, z, mt, pm, pt, weights):
    acts = (m2, at, bt, z, mt, pm, pt)
    outs = [(HD, RB, SQ), (TI, RB, RB)]
    return pl.pallas_call(
        pair_kernel,
        grid=(1,),
        out_shape=[jax.ShapeDtypeStruct(s, BF) for s in outs],
        in_specs=[full(a.shape) for a in acts] + [layer_of(w.shape, layer) for w in weights],
        out_specs=[full(s) for s in outs],
        scratch_shapes=[
            pltpu.VMEM((ND, HD, TI, SQ), BF),
            pltpu.VMEM((TI, 1024, RB), BF),
            pltpu.VMEM((RB, 1024), BF),
            pltpu.VMEM((2048, RB), F32),
            pltpu.VMEM((2048, RB), F32),
            pltpu.VMEM((2048, RB), F32),
            pltpu.VMEM((RB, TI, RB), BF),
            pltpu.VMEM((ND, RB, TI, RB), BF),
            pltpu.VMEM((ND, RB, TI, RB), BF),
            pltpu.VMEM((TI, RB, RB), F32),
            pltpu.VMEM((TI, RB, RB), BF),
            pltpu.VMEM((2, ND, TI, TI, RB), BF),
            pltpu.VMEM((RB, RB), F32),
            pltpu.VMEM((2, ND, 4, TI, RB), BF),
            pltpu.VMEM((4, RB, RB), F32),
            pltpu.VMEM((384, RB), BF),
            pltpu.VMEM((512, RB), BF),
            pltpu.VMEM((ND, TI, TI, RB), BF),
            pltpu.VMEM((TI, RB, RB), BF),
            pltpu.VMEM((ND, TI, HD, SQ), BF),
            pltpu.VMEM((2, 4096, RB), F32),
            pltpu.SemaphoreType.DMA((3, 13)), pltpu.SemaphoreType.DMA((3, 13)),
            pltpu.SemaphoreType.DMA((48,)), pltpu.SemaphoreType.DMA((48,)),
        ],
        compiler_params=params(2 + 2 * layer),
    )(*acts, *weights)


def solution(mesh):
    row_spec = P(('req', 'dap'))

    def local_body(m, z, mm, pm, *weights):
        (row_qkvg, row_bias, row_out, col_qkvg, col_out, mtr_in, mtr_out, opm_proj, opm_out) = weights[:9]
        mt, pt = run_masks(mm, pm)
        rmask = mm.astype(F32)
        pmask = pm.astype(F32)
        for layer in range(weights[0].shape[0]):
            m2, at, bt = run_msa(layer, m, z, rmask, mt, (row_qkvg, row_bias, row_out, col_qkvg, col_out, mtr_in, mtr_out, opm_proj))
            m, z = run_pair(layer, m2, at, bt, z, mt, pmask, pt, (opm_out,) + weights[9:])
        return m, z

    def run_blocks(*arrays):
        n_weights = len(arrays) - 4
        return jax.shard_map(local_body, mesh=mesh, in_specs=(row_spec,) * 4 + (P(),) * n_weights,
                             out_specs=(row_spec, row_spec), check_vma=False)(*arrays)

    return run_blocks
```

time: 1120 us -> 982 us (0.88)
  Pallas kernels: 0 us -> 968 us
  waiting for transfers between devices: 313 us -> 0 us
  matrix products: 247 us -> 0 us
  blocking collectives: 234 us -> 0 us
  local copies, waits for them, and re-layouts: 203 us -> 9.85 us
  starting transfers between devices: 47.4 us -> 0 us
  other arithmetic: 49.9 us -> 2.62 us
  between operations: 16.2 us -> 0.68 us
    pallas_call x0 -> x5, Pallas kernels: none -> 968 us  [the longest x2 544 us: run_pair(): pl.pallas_call(pair_kernel, grid=(1,), out_shape=[jax.ShapeDtypeStruct(s,...]
    dot_general x53 -> x0, matrix products: 163 us -> none  [the longest x32 75.3 us: dense(): jnp.einsum('...c,cf->...f', x, weight, preferred_element_type=jnp.float32)]
    all_to_all x8 -> x0, waiting for transfers between devices: 161 us -> none  [the longest x2 78.7 us: evoformer_block(): value_a7 = lax.all_to_all(array_b7, GROUP_AXIS, 0, 1, tiled=True)]
    all_gather x6 -> x0, waiting for transfers between devices: 152 us -> none  [the longest x4 110 us: pair_stack(): right_full = lax.all_gather(right_act, GROUP_AXIS, axis=0, tiled=True)]
    all_gather x8 -> x0, blocking collectives: 151 us -> none  [the longest x4 92.6 us: tri_attention(): lax.all_gather(head_bias(pair_norm, w_bias), GROUP_AXIS, axis=1, tiled=True)]
    sub x8 -> x0, matrix products: 84 us -> none  [attend(): attn_prob = jax.nn.softmax(logits, axis=-1).astype(jnp.bfloat16)]
    all_to_all x2 -> x0, blocking collectives: 83.4 us -> none  [the longest x1 51.6 us: evoformer_block(): array_b7 = lax.all_to_all(value_a7, GROUP_AXIS, 1, 0, tiled=True)]
    slice x20 -> x0, local copies, waits for them, and re-layouts: 62.6 us -> none  [the longest x12 35 us: attend(): keyvals[..., :head_width].reshape(n_batch, k_len, num_heads, head_dim)]
  transfers between devices with their start and end apart: 14 -> 0, of which waited for: 11 -> 0; matrix products, arithmetic and copies ran while one was open for 5% -> 0% of each run, Pallas kernels for 0% -> 0%
where the time goes in v1:
time: 982 us
  Pallas kernels  968 us (99%)
  local copies, waits for them, and re-layouts  9.85 us (1%)
    pallas_call x2, Pallas kernels, run_pair(): pl.pallas_call(pair_kernel, grid=(1,), out_shape=[jax.ShapeDtypeStruct(s,...  544 us
    pallas_call x2, Pallas kernels, run_msa(): pl.pallas_call(msa_kernel, grid=(1,), out_shape=[jax.ShapeDtypeStruct(s,...  414 us

profile of v1, /device:TPU:27, one launch (start us, length us, event | category | flops | bytes accessed | tf_op | source)
XLA Modules:
  0.0 981.5 jit_solution(6755804048445650156)
XLA Ops:
  0.6 1.3 convert_element_type.7.pm_ref
  1.9 1.3 convert_element_type.6.rmask_ref
  3.2 1.4 copy.27.row_b
  4.7 1.4 copy.29.tas_b
  6.1 1.4 copy.30.tae_b
  7.5 1.6 copy.28.opm_p
  9.1 10.0 %shard_map.248 = (f32[128,256]{1,0:T(8,128)}, f32[128,128]{1,0:T(8,128)}) custom-call(s32[32,128]{1,0:T(8,128)} %mm_ref.1, s32[16,128]{1,0:T(8,128)} %pm_ref.1), custom_call_target="tpu_custom_call" | custom-call | tf_op jit(solution)/shard_map/pallas_call | solution.py:538
  19.2 207.3 %shard_map.249 = (bf16[16,256,256]{2,1,0:T(8,128)(2,1)}, bf16[16,32,256]{2,1,0:T(8,128)(2,1)}, bf16[32,16,256]{2,1,0:T(8,128)(2,1)}) custom-call(bf16[32,128,256]{2,1,0:T(8,128)(2,1)} %m_ref.1, bf16[16,128,128]{2,1,0:T(8,128)(2,1)} %z_ref.3, f32[32,128]{1,0:T(8,128)} %convert_element_type.6.rmask_ref, f32[128,256]{1,0:T(8,128)} %get-tuple-element.12.mt_ref, ...), custom_call_target="tpu_custom_call" | custom-call | tf_op jit(solution)/shard_map/pallas_call | solution.py:553
  226.5 272.0 %shard_map.250 = (bf16[32,128,256]{2,1,0:T(8,128)(2,1)}, bf16[16,128,128]{2,1,0:T(8,128)(2,1)}) custom-call(bf16[16,256,256]{2,1,0:T(8,128)(2,1)} %get-tuple-element.13.m2_ref, bf16[16,32,256]{2,1,0:T(8,128)(2,1)} %get-tuple-element.14.at_ref, bf16[32,16,256]{2,1,0:T(8,128)(2,1)} %get-tuple-element.15.bt_ref, bf16[16,128,128]{2,1,0:T(8,128)(2,1)} %z_ref.3, ...), custom_call_target="tpu_custom_call" | custom-call | tf_op jit(solution)/shard_map/pallas_call | solution.py:578
  498.5 207.0 %shard_map.251 = (bf16[16,256,256]{2,1,0:T(8,128)(2,1)}, bf16[16,32,256]{2,1,0:T(8,128)(2,1)}, bf16[32,16,256]{2,1,0:T(8,128)(2,1)}) custom-call(bf16[32,128,256]{2,1,0:T(8,128)(2,1)} %get-tuple-element.17.m_ref, bf16[16,128,128]{2,1,0:T(8,128)(2,1)} %get-tuple-element.18.z_ref, f32[32,128]{1,0:T(8,128)} %convert_element_type.6.rmask_ref, ...), custom_call_target="tpu_custom_call" | custom-call | tf_op jit(solution)/shard_map/pallas_call | solution.py:553
  705.6 272.0 %shard_map.252 = (bf16[32,128,256]{2,1,0:T(8,128)(2,1)}, bf16[16,128,128]{2,1,0:T(8,128)(2,1)}) custom-call(bf16[16,256,256]{2,1,0:T(8,128)(2,1)} %get-tuple-element.19.m2_ref, bf16[16,32,256]{2,1,0:T(8,128)(2,1)} %get-tuple-element.20.at_ref, bf16[32,16,256]{2,1,0:T(8,128)(2,1)} %get-tuple-element.21.bt_ref, bf16[16,128,128]{2,1,0:T(8,128)(2,1)} %get-tuple-element.18.z_ref, ...), custom_call_target="tpu_custom_call" | custom-call | tf_op jit(solution)/shard_map/pallas_call | solution.py:578
  977.5 0.0 copy-start
  977.5 3.2 copy.37
  980.7 0.0 copy-done
  980.7 0.8 copy.38
Async XLA Ops:
  977.5 3.2 copy-start

commit v2 on v1

--- a/solution.py
+++ b/solution.py
@@ -176,39 +176,66 @@
     return jnp.broadcast_to(row, (RB, row.shape[1])).T
 
 
-def attend_tile(xn, wt_ref, wk, w_out, heads, bias_ref, key_mask):
-    length = xn.shape[0]
+def attend_tiles(xns, wt_ref, wk, w_out, heads, bias_ref, key_masks, depth):
+    length = xns[0].shape[0]
     width = heads * HD
-    proj = dot_nt(wt_ref[...], xn)
-    q_t = proj[:width].astype(BF)
-    v_t = proj[width:2 * width].astype(BF)
-    gate = jax.nn.sigmoid(proj[2 * width:].astype(BF).astype(F32))
-    keys = dot(xn, wk).astype(BF)
-    valid = key_mask > 0
+    projs = [dot_nt(wt_ref[...], xn) for xn in xns]
+    keys = [dot(xn, wk).astype(BF) for xn in xns]
+    q_t = [proj[:width].astype(BF) for proj in projs]
+    v_t = [proj[width:2 * width].astype(BF) for proj in projs]
+    gate = [jax.nn.sigmoid(proj[2 * width:].astype(BF).astype(F32)) for proj in projs]
+    valid = [key_mask > 0 for key_mask in key_masks]
     scale = HD ** -0.5 * LOG2E
-    pieces = []
-    for qc in range(length // RB):
-        outs = []
-        for h in range(heads):
-            hh = h % 4
-            q_h = q_t[HD * h:HD * h + HD, RB * qc:RB * qc + RB]
-            rhs = [q_h]
-            if hh > 0:
-                rhs = [jnp.zeros((HD * hh, RB), BF)] + rhs
-            if hh < 3:
-                rhs = rhs + [jnp.zeros((96 - HD * hh, RB), BF)]
-            logits = dot(keys[:, RB * (h // 4):RB * (h // 4) + RB], jnp.concatenate(rhs, 0)) * scale
-            if bias_ref is not None:
-                logits = logits + bias_ref[h]
-            logits = jnp.where(valid, logits, NEG)
-            top = jnp.max(logits, axis=0, keepdims=True)
-            e = jnp.exp2(logits - top)
-            inv = 1.0 / jnp.sum(e, axis=0, keepdims=True)
-            prob = (e * inv).astype(BF)
-            outs.append(dot(v_t[HD * h:HD * h + HD], prob))
-        gated = (jnp.concatenate(outs, 0) * gate[:, RB * qc:RB * qc + RB]).astype(BF)
-        pieces.append(dot_tn(gated, w_out))
-    return pieces
+
+    def logits_of(unit):
+        t, qc, h = unit
+        hh = h % 4
+        rhs = [q_t[t][HD * h:HD * h + HD, RB * qc:RB * qc + RB]]
+        if hh > 0:
+            rhs = [jnp.zeros((HD * hh, RB), BF)] + rhs
+        if hh < 3:
+            rhs = rhs + [jnp.zeros((96 - HD * hh, RB), BF)]
+        return dot(keys[t][:, RB * (h // 4):RB * (h // 4) + RB], jnp.concatenate(rhs, 0))
+
+    def prob_of(unit, raw):
+        t, qc, h = unit
+        logits = raw * scale
+        if bias_ref is not None:
+            logits = logits + bias_ref[h]
+        logits = jnp.where(valid[t], logits, NEG)
+        e = jnp.exp2(logits - jnp.max(logits, axis=0, keepdims=True))
+        return (e * (1.0 / jnp.sum(e, axis=0, keepdims=True))).astype(BF)
+
+    blocks = [(t, qc) for t in range(len(xns)) for qc in range(length // RB)]
+    units = [(t, qc, h) for t, qc in blocks for h in range(heads)]
+    raws = {i: logits_of(units[i]) for i in range(min(depth, len(units)))}
+    outs, probs, upds = {}, {}, {}
+
+    def flush(i):
+        t, qc, h = units[i]
+        outs[units[i]] = dot(v_t[t][HD * h:HD * h + HD], probs.pop(i))
+        if h == heads - 1:
+            o = jnp.concatenate([outs.pop((t, qc, hh)) for hh in range(heads)], 0)
+            upds[t, qc] = (o * gate[t][:, RB * qc:RB * qc + RB]).astype(BF)
+
+    for i in range(len(units)):
+        if i + depth < len(units):
+            raws[i + depth] = logits_of(units[i + depth])
+        probs[i] = prob_of(units[i], raws.pop(i))
+        if i > 0:
+            flush(i - 1)
+    flush(len(units) - 1)
+    pieces = [dot_tn(upds[block], w_out) for block in blocks]
+    per = length // RB
+    return [jnp.concatenate(pieces[t * per:t * per + per], 0) for t in range(len(xns))]
+
+
+def tile_loop(count, width, body):
+    def step(g, carry):
+        body([g * width + u for u in range(width)])
+        return carry
+
+    lax.fori_loop(0, count // width, step, 0)
 
 
 def prep_qkvg(w_ref, wt_ref, width):
@@ -241,12 +268,12 @@
     wb = jnp.concatenate([row_b[0], jnp.zeros((RB, 120), BF)], 1)
     wb_t = transpose_bf(wb)[0:8]
 
-    def bias_row(i, carry):
-        xn = norm_lanes(z_ref[i].astype(F32))
-        bscr[pl.ds(i, 8, stride=TI), :] = dot_nt(wb_t, xn)
-        return carry
-
-    lax.fori_loop(0, TI, bias_row, 0)
+    def bias_row(tiles):
+        rows = [dot_nt(wb_t, norm_lanes(z_ref[i].astype(F32))) for i in tiles]
+        for i, row in zip(tiles, rows):
+            bscr[pl.ds(i, 8, stride=TI), :] = row
+
+    tile_loop(TI, 8, bias_row)
     ball[me] = bscr[...].astype(BF).reshape(8, TI, RB)
     ex_b = Direct(me, lambda peer: ball.at[me], lambda owner: ball.at[owner], ssem, rsem, 0)
     ex_b.start()
@@ -257,19 +284,18 @@
         bias_t[h] = ball[:, h].reshape(RB, RB).astype(F32).T * LOG2E
     row_k = row_w[0, :, SQ:512]
     row_ow = row_o[0]
-    exchanges = []
     for ck in range(2):
-        def row_body(sl, carry):
-            s = ck * TI + sl
-            x = m_ref[s]
-            key_mask = column_of(rmask_ref[pl.ds(s, 1), :])
-            upd, = attend_tile(norm_lanes(x.astype(F32)), wt, row_k, row_ow, 8, bias_t, key_mask)
-            y = residual(x, upd).astype(F32)
-            for half in range(2):
-                scr[half, pl.ds(sl, RB, stride=TI), :] = y[:, RB * half:RB * half + RB]
-            return carry
-
-        lax.fori_loop(0, TI, row_body, 0)
+        def row_body(sls):
+            xs = [m_ref[ck * TI + sl] for sl in sls]
+            masks = [column_of(rmask_ref[pl.ds(ck * TI + sl, 1), :]) for sl in sls]
+            xns = [norm_lanes(x.astype(F32)) for x in xs]
+            upds = attend_tiles(xns, wt, row_k, row_ow, 8, bias_t, masks, 4)
+            for sl, x, upd in zip(sls, xs, upds):
+                y = residual(x, upd).astype(F32)
+                for half in range(2):
+                    scr[half, pl.ds(sl, RB, stride=TI), :] = y[:, RB * half:RB * half + RB]
+
+        tile_loop(TI, 2, row_body)
 
         def pack(d, carry):
             for half in range(2):
@@ -278,36 +304,55 @@
             return carry
 
         lax.fori_loop(0, 8, pack, 0)
-        ex = Direct(me, lambda peer: sendbuf.at[ck, peer], lambda owner: rbuf.at[owner * 2 + ck], ssem, rsem, 8 * (ck + 1))
-        ex.start()
-        exchanges.append(ex)
         rbuf[me * 2 + ck] = sendbuf[ck, me]
+        if ck == 0:
+            ex0 = Direct(me, lambda peer: sendbuf.at[0, peer], lambda owner: rbuf.at[owner * 2], ssem, rsem, ND)
+            ex0.start()
+
+    def quarter(q):
+        part = pl.ds(pl.multiple_of(q * 4, 4), 4)
+        return Direct(me, lambda peer: sendbuf.at[1, peer, part], lambda owner: rbuf.at[owner * 2 + 1, part], ssem, rsem, ND * 2 + q * ND)
+
+    for q in range(4):
+        quarter(q).start()
     ex_b.wait_send()
     prep_qkvg(col_w, wt, SQ)
-    for ex in exchanges:
-        ex.wait_recv()
+    ex0.wait_recv()
     col_k = col_w[0, :, SQ:512]
     col_ow = col_o[0]
 
-    def col_body(r, carry):
-        x = rbuf[:, r].reshape(SQ, SQ)
-        mrow = mt_ref[pl.ds(me * TI + r, 1), :]
-        key_mask = column_of(mrow)
-        upd = attend_tile(norm_lanes(x.astype(F32)), wt, col_k, col_ow, 8, None, key_mask)
-        y = residual(x, jnp.concatenate(upd, 0))
-        hid = jnp.maximum(dot(norm_lanes(y.astype(F32)), mtr_i[0]), 0.0).astype(BF)
-        y2 = residual(y, dot(hid, mtr_o[0]))
-        m2_ref[r] = y2
-        ab = dot_nt(opt[...], norm_lanes(y2.astype(F32))).astype(BF).astype(F32) * mrow
-        at_ref[r] = ab[0:HD].astype(BF)
-        for half in range(2):
-            scr[half, pl.ds(r, HD, stride=TI), :] = ab[HD:64, RB * half:RB * half + RB]
+    def col_body(rs):
+        xs = [rbuf[:, r].reshape(SQ, SQ) for r in rs]
+        mrows = [mt_ref[pl.ds(me * TI + r, 1), :] for r in rs]
+        masks = [column_of(mrow) for mrow in mrows]
+        upds = attend_tiles([norm_lanes(x.astype(F32)) for x in xs], wt, col_k, col_ow, 8, None, masks, 2)
+        for r, x, upd in zip(rs, xs, upds):
+            m2_ref[r] = residual(x, upd)
+
+    def mtr_body(rs):
+        ys = [m2_ref[r] for r in rs]
+        mrows = [mt_ref[pl.ds(me * TI + r, 1), :] for r in rs]
+        xns = [norm_lanes(y.astype(F32)) for y in ys]
+        hids = [jnp.maximum(dot(xn, mtr_i[0]), 0.0).astype(BF) for xn in xns]
+        y2s = [residual(y, dot(hid, mtr_o[0])) for y, hid in zip(ys, hids)]
+        xns = [norm_lanes(y2.astype(F32)) for y2 in y2s]
+        abs_ = [dot_nt(opt[...], xn).astype(BF).astype(F32) * mrow for xn, mrow in zip(xns, mrows)]
+        for r, y2, ab in zip(rs, y2s, abs_):
+            m2_ref[r] = y2
+            at_ref[r] = ab[0:HD].astype(BF)
+            for half in range(2):
+                scr[half, pl.ds(r, HD, stride=TI), :] = ab[HD:2 * HD, RB * half:RB * half + RB]
+
+    def col_quarter(q, carry):
+        quarter(q).wait_recv()
+        tile_loop(4, 1, lambda rs: col_body([q * 4 + r for r in rs]))
+        tile_loop(4, 2, lambda rs: mtr_body([q * 4 + r for r in rs]))
         return carry
 
-    lax.fori_loop(0, TI, col_body, 0)
+    lax.fori_loop(0, 4, col_quarter, 0)
     for half in range(2):
         bt_ref[:, :, RB * half:RB * half + RB] = scr[half, 0:512, :].astype(BF).reshape(HD, TI, RB)
-    for ex in exchanges:
+    for ex in [ex0] + [quarter(q) for q in range(4)]:
         ex.wait_send()
 
 
@@ -339,56 +384,66 @@
 
     left = at_ref[...].reshape(512, SQ)
 
-    def opm_e(e, carry):
-        rhs = btall[:, e].reshape(RB, SQ)
-        o = dot_nt(left, rhs).astype(BF).reshape(TI, HD, RB)
-        obuf[:, pl.ds(pl.multiple_of(e * HD, HD), HD), :] = o
-        return carry
-
-    lax.fori_loop(0, HD, opm_e, 0)
+    def opm_e(es):
+        rhs = [btall[:, e].reshape(RB, SQ) for e in es]
+        os_ = [dot_nt(left, r).astype(BF).reshape(TI, HD, RB) for r in rhs]
+        for e, o in zip(es, os_):
+            obuf[:, pl.ds(pl.multiple_of(e * HD, HD), HD), :] = o
+
+    tile_loop(HD, 2, opm_e)
 
     ex_m = Direct(me, lambda peer: m2_ref.at[:, pl.ds(pl.multiple_of(peer * HD, HD), HD), :], lambda owner: mrecv.at[owner], ds, dr, 0)
     mrecv[me] = m2_ref[:, pl.ds(pl.multiple_of(me * HD, HD), HD), :]
     ex_m.start([1, 2])
 
-    def opm_i(i, carry):
-        y_t = dot(opw[...], obuf[i]) * scr_x[pl.ds(i, 1), :]
-        z1[i] = residual(z_ref[i], y_t.T)
-        return carry
-
-    lax.fori_loop(0, TI, opm_i, 0)
+    def opm_i(tiles):
+        y_ts = [dot(opw[...], obuf[i]) * scr_x[pl.ds(i, 1), :] for i in tiles]
+        outs = [residual(z_ref[i], y_t.T) for i, y_t in zip(tiles, y_ts)]
+        for i, out in zip(tiles, outs):
+            z1[i] = out
+
+    tile_loop(TI, 4, opm_i)
 
     def front(w_ref, z_src, ball, left_too):
         wt_l = twt
         wt_l[...] = transpose_bf(w_ref[0, :, 0:512])
         wg = w_ref[0, :, 512:640]
 
-        def body(i, carry):
-            xn = norm_lanes(z_src[i].astype(F32))
-            mrow = pm_ref[pl.ds(i, 1), :]
+        def body(tiles):
+            xns = [norm_lanes(z_src[i].astype(F32)) for i in tiles]
+            mrows = [pm_ref[pl.ds(i, 1), :] for i in tiles]
             if left_too:
-                pr = dot_nt(wt_l[...], xn)
-                scr_a[pl.ds(i, RB, stride=TI), :] = mrow * jax.nn.sigmoid(pr[SQ:384]) * pr[0:RB]
-                pb, pg = pr[RB:SQ], pr[384:512]
+                prs = [dot_nt(wt_l[...], xn) for xn in xns]
+                lefts = [mrow * jax.nn.sigmoid(pr[SQ:384]) * pr[0:RB] for mrow, pr in zip(mrows, prs)]
+                pbs = [pr[RB:SQ] for pr in prs]
+                pgs = [pr[384:512] for pr in prs]
             else:
-                pb = dot_nt(wt_l[RB:SQ, :], xn)
-                pg = dot_nt(wt_l[384:512, :], xn)
-            scr_b[pl.ds(i, RB, stride=TI), :] = mrow * jax.nn.sigmoid(pg) * pb
-            gbuf[i] = jax.nn.sigmoid(dot(xn, wg))
-            return carry
-
-        lax.fori_loop(0, TI, body, 0)
+                lefts = []
+                pbs = [dot_nt(wt_l[RB:SQ, :], xn) for xn in xns]
+                pgs = [dot_nt(wt_l[384:512, :], xn) for xn in xns]
+            gates = [dot(xn, wg) for xn in xns]
+            rights = [mrow * jax.nn.sigmoid(pg) * pb for mrow, pg, pb in zip(mrows, pgs, pbs)]
+            gates = [jax.nn.sigmoid(g) for g in gates]
+            for i, left in zip(tiles, lefts):
+                scr_a[pl.ds(i, RB, stride=TI), :] = left
+            for i, right, gate in zip(tiles, rights, gates):
+                scr_b[pl.ds(i, RB, stride=TI), :] = right
+                gbuf[i] = gate
+
+        tile_loop(TI, 4, body)
         ball[me] = scr_b[...].astype(BF).reshape(RB, TI, RB)
 
     def finish(w_ref, z_src, z_dst):
         w = w_ref[0]
 
-        def body(i, carry):
-            xn = norm_rows(scr_x[pl.ds(i, RB, stride=TI), :])
-            z_dst[i] = residual(z_src[i], gbuf[i] * dot_tn(xn, w))
-            return carry
-
-        lax.fori_loop(0, TI, body, 0)
+        def body(tiles):
+            xns = [norm_rows(scr_x[pl.ds(i, RB, stride=TI), :]) for i in tiles]
+            ys = [dot_tn(xn, w) for xn in xns]
+            outs = [residual(z_src[i], gbuf[i] * y) for i, y in zip(tiles, ys)]
+            for i, out in zip(tiles, outs):
+                z_dst[i] = out
+
+        tile_loop(TI, 4, body)
 
     front(tmo_p, z1, ball1, True)
     ag1 = Chain(me, ball1, ch_s.at[1], ch_r.at[1])
@@ -415,15 +470,16 @@
     ex_z1.wait_recv()
     scr_b[...] = zcol[0].astype(F32).reshape(2048, RB)
 
-    def in_left(i, carry):
-        xn = norm_lanes(scr_b[pl.ds(i, RB, stride=TI), :])
-        mrow = pt_ref[pl.ds(me * TI + i, 1), :]
-        pa = dot_nt(twt[0:RB, :], xn)
-        pg = dot_nt(twt[SQ:384, :], xn)
-        scr_a[pl.ds(i, RB, stride=TI), :] = mrow * jax.nn.sigmoid(pg) * pa
-        return carry
-
-    lax.fori_loop(0, TI, in_left, 0)
+    def in_left(tiles):
+        xns = [norm_lanes(scr_b[pl.ds(i, RB, stride=TI), :]) for i in tiles]
+        mrows = [pt_ref[pl.ds(me * TI + i, 1), :] for i in tiles]
+        pas = [dot_nt(twt[0:RB, :], xn) for xn in xns]
+        pgs = [dot_nt(twt[SQ:384, :], xn) for xn in xns]
+        lefts = [mrow * jax.nn.sigmoid(pg) * pa for mrow, pg, pa in zip(mrows, pgs, pas)]
+        for i, left in zip(tiles, lefts):
+            scr_a[pl.ds(i, RB, stride=TI), :] = left
+
+    tile_loop(TI, 4, in_left)
     a_c[...] = scr_a[...].astype(BF).reshape(RB, TI, RB)
     ag2.finish()
 
@@ -441,11 +497,12 @@
     def tri_bias(w_ref, tile, slot, base):
         wb_t = transpose_bf(jnp.concatenate([w_ref[0], jnp.zeros((RB, 124), BF)], 1))[0:8]
 
-        def body(i, carry):
-            sbias[pl.ds(i, 8, stride=TI), :] = dot_nt(wb_t, norm_lanes(tile(i)))
-            return carry
-
-        lax.fori_loop(0, TI, body, 0)
+        def body(tiles):
+            rows = [dot_nt(wb_t, norm_lanes(tile(i))) for i in tiles]
+            for i, row in zip(tiles, rows):
+                sbias[pl.ds(i, 8, stride=TI), :] = row
+
+        tile_loop(TI, 8, body)
         ball3[slot, me] = sbias[0:64, :].astype(BF).reshape(4, TI, RB)
         ex = Direct(me, lambda peer: ball3.at[slot, me], lambda owner: ball3.at[slot, owner], ds, dr, base)
         ex.start()
@@ -461,13 +518,14 @@
     take_bias(0)
     tas_k = tas_w[0, :, RB:SQ]
 
-    def tas_body(i, carry):
-        x = z1[i]
-        upd, = attend_tile(norm_lanes(x.astype(F32)), wt, tas_k, tas_o[0], 4, bias_t, column_of(pm_ref[pl.ds(i, 1), :]))
-        z1[i] = residual(x, upd)
-        return carry
-
-    lax.fori_loop(0, TI, tas_body, 0)
+    def tas_body(tiles):
+        xs = [z1[i] for i in tiles]
+        masks = [column_of(pm_ref[pl.ds(i, 1), :]) for i in tiles]
+        upds = attend_tiles([norm_lanes(x.astype(F32)) for x in xs], wt, tas_k, tas_o[0], 4, bias_t, masks, 4)
+        for i, x, upd in zip(tiles, xs, upds):
+            z1[i] = residual(x, upd)
+
+    tile_loop(TI, 4, tas_body)
 
     ex_z2 = Direct(me, lambda peer: z1.at[:, pl.ds(pl.multiple_of(peer * TI, TI), TI), :], lambda owner: zcol.at[1, owner], ds, dr, 24)
     ex_z2.start()
@@ -480,13 +538,14 @@
     take_bias(1)
     tae_k = tae_w[0, :, RB:SQ]
 
-    def tae_body(i, carry):
-        x = scr_b[pl.ds(i, RB, stride=TI), :]
-        upd, = attend_tile(norm_lanes(x), wt, tae_k, tae_o[0], 4, bias_t, column_of(pt_ref[pl.ds(me * TI + i, 1), :]))
-        scr_a[pl.ds(i, RB, stride=TI), :] = x + upd
-        return carry
-
-    lax.fori_loop(0, TI, tae_body, 0)
+    def tae_body(tiles):
+        xs = [scr_b[pl.ds(i, RB, stride=TI), :] for i in tiles]
+        masks = [column_of(pt_ref[pl.ds(me * TI + i, 1), :]) for i in tiles]
+        upds = attend_tiles([norm_lanes(x) for x in xs], wt, tae_k, tae_o[0], 4, bias_t, masks, 4)
+        for i, x, upd in zip(tiles, xs, upds):
+            scr_a[pl.ds(i, RB, stride=TI), :] = x + upd
+
+    tile_loop(TI, 4, tae_body)
     zsend[...] = scr_a[...].astype(BF).reshape(8, TI, TI, RB)
     ex_z3 = Direct(me, lambda peer: zsend.at[peer], lambda owner: z4.at[:, pl.ds(pl.multiple_of(owner * TI, TI), TI), :], ds, dr, 40)
     ex_z3.start()
@@ -502,21 +561,23 @@
 
     lax.fori_loop(0, 8, widen, 0)
 
-    def take_seq(s, carry):
-        for half in range(2):
-            mout_ref[s, :, RB * half:RB * half + RB] = mscr[half, pl.ds(s, RB, stride=HD), :].astype(BF)
-        return carry
-
-    lax.fori_loop(0, HD, take_seq, 0)
+    def take_seq(seqs):
+        for s in seqs:
+            for half in range(2):
+                mout_ref[s, :, RB * half:RB * half + RB] = mscr[half, pl.ds(s, RB, stride=HD), :].astype(BF)
+
+    tile_loop(HD, 4, take_seq)
     ex_z3.wait_recv()
 
-    def trans(i, carry):
-        x = z4[i]
-        hid = jnp.maximum(dot(norm_lanes(x.astype(F32)), ptr_i[0]), 0.0).astype(BF)
-        zout_ref[i] = residual(x, dot(hid, ptr_o[0]))
-        return carry
-
-    lax.fori_loop(0, TI, trans, 0)
+    def trans(tiles):
+        xs = [z4[i] for i in tiles]
+        xns = [norm_lanes(x.astype(F32)) for x in xs]
+        hids = [jnp.maximum(dot(xn, ptr_i[0]), 0.0).astype(BF) for xn in xns]
+        outs = [residual(x, dot(hid, ptr_o[0])) for x, hid in zip(xs, hids)]
+        for i, out in zip(tiles, outs):
+            zout_ref[i] = out
+
+    tile_loop(TI, 4, trans)
     for ex in (ag0, ag1, ag2, ex_m, ex_s, ex_e, ex_z2, ex_z3):
         ex.wait_send()
 
@@ -566,7 +627,7 @@
             pltpu.VMEM((2, ND, TI, TI, SQ), BF),
             pltpu.VMEM((2 * ND, TI, TI, SQ), BF),
             pltpu.VMEM((RB, RB), F32),
-            pltpu.SemaphoreType.DMA((24,)), pltpu.SemaphoreType.DMA((24,)),
+            pltpu.SemaphoreType.DMA((48,)), pltpu.SemaphoreType.DMA((48,)),
         ],
         compiler_params=params(1 + 2 * layer),
     )(*acts, *weights)

time: 982 us -> 682 us (0.69)
  Pallas kernels: 968 us -> 668 us
    pallas_call x2, Pallas kernels: 414 us -> 214 us  [run_msa(): pl.pallas_call(msa_kernel, grid=(1,), out_shape=[jax.ShapeDtypeStruct(s,...]
    pallas_call x2, Pallas kernels: 544 us -> 444 us  [run_pair(): pl.pallas_call(pair_kernel, grid=(1,), out_shape=[jax.ShapeDtypeStruct(s,...]
where the time goes in v2:
time: 682 us; the launch traced here: 681 us
  Pallas kernels  668 us (98%)
  local copies, waits for them, and re-layouts  9.85 us (1%)
    pallas_call x2, Pallas kernels, run_pair(): pl.pallas_call(pair_kernel, grid=(1,), out_shape=[jax.ShapeDtypeStruct(s,...  444 us
    pallas_call x2, Pallas kernels, run_msa(): pl.pallas_call(msa_kernel, grid=(1,), out_shape=[jax.ShapeDtypeStruct(s,...  214 us

profile of v2, /device:TPU:27, one launch (start us, length us, event | category | flops | bytes accessed | tf_op | source)
XLA Modules:
  0.0 680.8 jit_solution(1301043121663938266)
XLA Ops:
  0.6 1.3 convert_element_type.7.pm_ref
  1.9 1.3 convert_element_type.6.rmask_ref
  3.2 1.4 copy.27.row_b
  4.7 1.4 copy.29.tas_b
  6.1 1.4 copy.30.tae_b
  7.5 1.6 copy.28.opm_p
  9.1 10.0 %shard_map.248 = (f32[128,256]{1,0:T(8,128)}, f32[128,128]{1,0:T(8,128)}) custom-call(s32[32,128]{1,0:T(8,128)} %mm_ref.1, s32[16,128]{1,0:T(8,128)} %pm_ref.1), custom_call_target="tpu_custom_call" | custom-call | tf_op jit(solution)/shard_map/pallas_call | solution.py:599
  19.2 107.0 %shard_map.249 = (bf16[16,256,256]{2,1,0:T(8,128)(2,1)}, bf16[16,32,256]{2,1,0:T(8,128)(2,1)}, bf16[32,16,256]{2,1,0:T(8,128)(2,1)}) custom-call(bf16[32,128,256]{2,1,0:T(8,128)(2,1)} %m_ref.1, bf16[16,128,128]{2,1,0:T(8,128)(2,1)} %z_ref.3, f32[32,128]{1,0:T(8,128)} %convert_element_type.6.rmask_ref, f32[128,256]{1,0:T(8,128)} %get-tuple-element.12.mt_ref, ...), custom_call_target="tpu_custom_call" | custom-call | tf_op jit(solution)/shard_map/pallas_call | solution.py:614
  126.2 222.1 %shard_map.250 = (bf16[32,128,256]{2,1,0:T(8,128)(2,1)}, bf16[16,128,128]{2,1,0:T(8,128)(2,1)}) custom-call(bf16[16,256,256]{2,1,0:T(8,128)(2,1)} %get-tuple-element.13.m2_ref, bf16[16,32,256]{2,1,0:T(8,128)(2,1)} %get-tuple-element.14.at_ref, bf16[32,16,256]{2,1,0:T(8,128)(2,1)} %get-tuple-element.15.bt_ref, bf16[16,128,128]{2,1,0:T(8,128)(2,1)} %z_ref.3, ...), custom_call_target="tpu_custom_call" | custom-call | tf_op jit(solution)/shard_map/pallas_call | solution.py:639
  348.2 106.6 %shard_map.251 = (bf16[16,256,256]{2,1,0:T(8,128)(2,1)}, bf16[16,32,256]{2,1,0:T(8,128)(2,1)}, bf16[32,16,256]{2,1,0:T(8,128)(2,1)}) custom-call(bf16[32,128,256]{2,1,0:T(8,128)(2,1)} %get-tuple-element.17.m_ref, bf16[16,128,128]{2,1,0:T(8,128)(2,1)} %get-tuple-element.18.z_ref, f32[32,128]{1,0:T(8,128)} %convert_element_type.6.rmask_ref, ...), custom_call_target="tpu_custom_call" | custom-call | tf_op jit(solution)/shard_map/pallas_call | solution.py:614
  454.9 221.9 %shard_map.252 = (bf16[32,128,256]{2,1,0:T(8,128)(2,1)}, bf16[16,128,128]{2,1,0:T(8,128)(2,1)}) custom-call(bf16[16,256,256]{2,1,0:T(8,128)(2,1)} %get-tuple-element.19.m2_ref, bf16[16,32,256]{2,1,0:T(8,128)(2,1)} %get-tuple-element.20.at_ref, bf16[32,16,256]{2,1,0:T(8,128)(2,1)} %get-tuple-element.21.bt_ref, bf16[16,128,128]{2,1,0:T(8,128)(2,1)} %get-tuple-element.18.z_ref, ...), custom_call_target="tpu_custom_call" | custom-call | tf_op jit(solution)/shard_map/pallas_call | solution.py:639
  676.8 0.0 copy-start
  676.8 3.2 copy.37
  680.0 0.0 copy-done
  680.0 0.8 copy.38
Async XLA Ops:
  676.8 3.2 copy-start

commit v3 on v2

--- a/solution.py
+++ b/solution.py
@@ -1,5 +1,3 @@
-import functools
-
 import jax
 import jax.numpy as jnp
 from jax import lax
@@ -93,83 +91,116 @@
         self.buf, self.ssem, self.rsem = buf, ssem, rsem
         self.z, self.c = lax.div(me, 2), lax.rem(me, 2)
         self.me, self.partner = me, me + 1 - 2 * self.c
-
-    def cp(self, slot, peer, sem):
-        return remote(self.buf.at[slot], self.buf.at[slot], self.ssem.at[sem], self.rsem.at[sem], peer)
+        self.size = buf.shape[1] // 2
+
+    def cp(self, slot, peer, sem, half):
+        ref = self.buf.at[slot, pl.ds(half * self.size, self.size)]
+        return remote(ref, ref, self.ssem.at[half, sem], self.rsem.at[half, sem], peer)
 
     def slot(self, off, other=False):
         core = 1 - self.c if other else self.c
         return (self.z + off) * 2 + core
 
+    def own(self, act):
+        for half in range(2):
+            @pl.when(self.z < 3)
+            def _():
+                act(self.cp(self.me, self.me + 2, 0, half))
+
+            @pl.when(self.z > 0)
+            def _():
+                act(self.cp(self.me, self.me - 2, 3, half))
+
+        for half in range(2):
+            act(self.cp(self.me, self.partner, 6, half))
+
+    def forward(self, t, half, before, act):
+        z = self.z
+
+        @pl.when(z >= t)
+        def _():
+            if before:
+                before(self.cp(self.slot(-t), self.me, t - 1, half))
+            if t < 3:
+                @pl.when(z < 3)
+                def _():
+                    act(self.cp(self.slot(-t), self.me + 2, t, half))
+            act(self.cp(self.slot(-t), self.partner, 6 + t, half))
+
+        @pl.when(z + t <= 3)
+        def _():
+            if before:
+                before(self.cp(self.slot(t), self.me, 2 + t, half))
+            if t < 3:
+                @pl.when(z > 0)
+                def _():
+                    act(self.cp(self.slot(t), self.me - 2, 3 + t, half))
+            act(self.cp(self.slot(t), self.partner, 9 + t, half))
+
     def start(self):
-        @pl.when(self.z < 3)
-        def _():
-            self.cp(self.me, self.me + 2, 0).start()
-
-        @pl.when(self.z > 0)
-        def _():
-            self.cp(self.me, self.me - 2, 3).start()
-
-        self.cp(self.me, self.partner, 6).start()
-
-    def finish(self):
+        self.own(lambda c: c.start())
+
+    def finish(self, hook=None):
         z = self.z
         for t in range(1, 4):
-            @pl.when(z >= t)
+            for half in range(2):
+                self.forward(t, half, lambda c: c.wait_recv(), lambda c: c.start())
+            if hook is not None:
+                hook(t)
+        for half in range(2):
+            self.cp(self.partner, self.me, 6, half).wait_recv()
+            for t in range(1, 4):
+                @pl.when(z >= t)
+                def _():
+                    self.cp(self.slot(-t, True), self.me, 6 + t, half).wait_recv()
+
+                @pl.when(z + t <= 3)
+                def _():
+                    self.cp(self.slot(t, True), self.me, 9 + t, half).wait_recv()
+
+    def wait_send(self):
+        self.own(lambda c: c.wait_send())
+        for t in range(1, 4):
+            for half in range(2):
+                self.forward(t, half, None, lambda c: c.wait_send())
+
+
+class Return:
+    def __init__(self, me, src, dst, ssem, rsem):
+        self.me, self.src, self.dst, self.ssem, self.rsem = me, src, dst, ssem, rsem
+        self.z, self.c = lax.div(me, 2), lax.rem(me, 2)
+
+    def copy_to(self, off, core):
+        peer = (self.z + off) * 2 + core
+        return remote(self.src(peer), self.dst(self.me), self.ssem.at[(off + 3) * 2 + core], self.rsem.at[(off + 3) * 2 + self.c], peer)
+
+    def start(self, off, cond, cores=(0, 1)):
+        @pl.when(cond)
+        def _():
+            for core in cores:
+                self.copy_to(off, core).start()
+
+    def start_partner(self):
+        self.copy_to(0, 1 - self.c).start()
+
+    def each(self, fn):
+        fn(0, 1 - self.c)
+        for off in (-3, -2, -1, 1, 2, 3):
+            @pl.when(jnp.logical_and(self.z + off >= 0, self.z + off <= 3))
             def _():
-                self.cp(self.slot(-t), self.me, t - 1).wait_recv()
-                if t < 3:
-                    @pl.when(z < 3)
-                    def _():
-                        self.cp(self.slot(-t), self.me + 2, t).start()
-                self.cp(self.slot(-t), self.partner, 6 + t).start()
-
-            @pl.when(z + t <= 3)
-            def _():
-                self.cp(self.slot(t), self.me, 3 + t - 1).wait_recv()
-                if t < 3:
-                    @pl.when(z > 0)
-                    def _():
-                        self.cp(self.slot(t), self.me - 2, 3 + t).start()
-                self.cp(self.slot(t), self.partner, 9 + t).start()
-        self.cp(self.partner, self.me, 6).wait_recv()
-        for t in range(1, 4):
-            @pl.when(z >= t)
-            def _():
-                self.cp(self.slot(-t, True), self.me, 6 + t).wait_recv()
-
-            @pl.when(z + t <= 3)
-            def _():
-                self.cp(self.slot(t, True), self.me, 9 + t).wait_recv()
+                for core in range(2):
+                    fn(off, core)
+
+    def wait_recv(self):
+        def one(off, core):
+            owner = (self.z + off) * 2 + core
+            sem = (3 - off) * 2 + core
+            remote(self.src(self.me), self.dst(owner), self.ssem.at[sem], self.rsem.at[sem], self.me).wait_recv()
+
+        self.each(one)
 
     def wait_send(self):
-        z = self.z
-
-        @pl.when(z < 3)
-        def _():
-            self.cp(self.me, self.me + 2, 0).wait_send()
-
-        @pl.when(z > 0)
-        def _():
-            self.cp(self.me, self.me - 2, 3).wait_send()
-
-        self.cp(self.me, self.partner, 6).wait_send()
-        for t in range(1, 4):
-            @pl.when(z >= t)
-            def _():
-                if t < 3:
-                    @pl.when(z < 3)
-                    def _():
-                        self.cp(self.slot(-t), self.me + 2, t).wait_send()
-                self.cp(self.slot(-t), self.partner, 6 + t).wait_send()
-
-            @pl.when(z + t <= 3)
-            def _():
-                if t < 3:
-                    @pl.when(z > 0)
-                    def _():
-                        self.cp(self.slot(t), self.me - 2, 3 + t).wait_send()
-                self.cp(self.slot(t), self.partner, 9 + t).wait_send()
+        self.each(lambda off, core: self.copy_to(off, core).wait_send())
 
 
 def column_of(row):
@@ -243,30 +274,40 @@
     wt_ref[width:3 * width, :] = transpose_bf(w_ref[0, :, 2 * width:4 * width])
 
 
-def mask_kernel(mm_ref, pm_ref, mt_ref, pt_ref, mbuf, pbuf, ssem, rsem):
+def blocks_kernel(m_in, z_in, mm_ref, pm_in,
+                  row_w, row_bt, row_o, col_w, col_o, mtr_i, mtr_o, opt, opm_o,
+                  tmo_p, tmo_o, tmi_p, tmi_o, tas_w, tas_bt, tas_o, tae_w, tae_bt, tae_o, ptr_i, ptr_o,
+                  mout_ref, zout_ref,
+                  mbuf, pbuf, mt_ref, pt_ref, rmask_ref, pm_ref,
+                  ball, bias_t, wt, scr, sendbuf, rbuf, bscr, m2_ref, at_ref,
+                  btall, obuf, opw, scr_a, scr_b, scr_x, a_c, ball1, ball2, gbuf, z1, zcol, sbias, ball3,
+                  wt2, twt, zsend, z4, mrecv, mscr,
+                  ssem, rsem, ch_s, ch_r, ms, mr):
     me = lax.axis_index('dap')
+    chip = lax.div(me, 2)
+    first = pl.program_id(0) == 0
     group_barrier(me)
-    mbuf[me] = mm_ref[...].astype(F32)
-    pbuf[me] = pm_ref[...].astype(F32)
-    ex_m = Direct(me, lambda peer: mbuf.at[me], lambda owner: mbuf.at[owner], ssem, rsem, 0)
-    ex_p = Direct(me, lambda peer: pbuf.at[me], lambda owner: pbuf.at[owner], ssem, rsem, ND)
-    ex_m.start()
-    ex_p.start()
-    ex_m.wait_recv()
-    ex_p.wait_recv()
-    mt_ref[...] = mbuf[...].reshape(SQ, RB).T
-    pt_ref[...] = pbuf[...].reshape(RB, RB).T
-    ex_m.wait_send()
-    ex_p.wait_send()
-
-
-def msa_kernel(m_ref, z_ref, rmask_ref, mt_ref, row_w, row_b, row_o, col_w, col_o, mtr_i, mtr_o, opm_p,
-               m2_ref, at_ref, bt_ref,
-               bloc, ball, bias_t, wt, opt, scr, sendbuf, rbuf, bscr, ssem, rsem):
-    me = lax.axis_index('dap')
-    group_barrier(me)
-    wb = jnp.concatenate([row_b[0], jnp.zeros((RB, 120), BF)], 1)
-    wb_t = transpose_bf(wb)[0:8]
+    ex_k = [Direct(me, lambda peer, buf=buf: buf.at[me], lambda owner, buf=buf: buf.at[owner], ssem, rsem, base)
+            for buf, base in ((mbuf, 104), (pbuf, 112))]
+
+    @pl.when(first)
+    def _():
+        rmask_ref[...] = mm_ref[...].astype(F32)
+        pm_ref[...] = pm_in[...].astype(F32)
+        mbuf[me] = rmask_ref[...]
+        pbuf[me] = pm_ref[...]
+        for ex in ex_k:
+            ex.start()
+
+        def take(s, carry):
+            mout_ref[s] = m_in[s]
+            return carry
+
+        lax.fori_loop(0, HD, take, 0)
+        zout_ref[...] = z_in[...]
+
+    m_ref, z_ref = mout_ref, zout_ref
+    wb_t = row_bt[0]
 
     def bias_row(tiles):
         rows = [dot_nt(wb_t, norm_lanes(z_ref[i].astype(F32))) for i in tiles]
@@ -275,10 +316,19 @@
 
     tile_loop(TI, 8, bias_row)
     ball[me] = bscr[...].astype(BF).reshape(8, TI, RB)
-    ex_b = Direct(me, lambda peer: ball.at[me], lambda owner: ball.at[owner], ssem, rsem, 0)
+    ex_b = Direct(me, lambda peer: ball.at[me], lambda owner: ball.at[owner], ssem, rsem, TI)
     ex_b.start()
     prep_qkvg(row_w, wt, SQ)
-    opt[...] = transpose_bf(jnp.concatenate([opm_p[0], jnp.zeros((SQ, 64), BF)], 1))[0:64]
+
+    @pl.when(first)
+    def _():
+        for ex in ex_k:
+            ex.wait_recv()
+        mt_ref[...] = mbuf[...].reshape(SQ, RB).T
+        pt_ref[...] = pbuf[...].reshape(RB, RB).T
+        for ex in ex_k:
+            ex.wait_send()
+
     ex_b.wait_recv()
     for h in range(8):
         bias_t[h] = ball[:, h].reshape(RB, RB).astype(F32).T * LOG2E
@@ -306,12 +356,12 @@
         lax.fori_loop(0, 8, pack, 0)
         rbuf[me * 2 + ck] = sendbuf[ck, me]
         if ck == 0:
-            ex0 = Direct(me, lambda peer: sendbuf.at[0, peer], lambda owner: rbuf.at[owner * 2], ssem, rsem, ND)
+            ex0 = Direct(me, lambda peer: sendbuf.at[0, peer], lambda owner: rbuf.at[owner * 2], ssem, rsem, 24)
             ex0.start()
 
     def quarter(q):
         part = pl.ds(pl.multiple_of(q * 4, 4), 4)
-        return Direct(me, lambda peer: sendbuf.at[1, peer, part], lambda owner: rbuf.at[owner * 2 + 1, part], ssem, rsem, ND * 2 + q * ND)
+        return Direct(me, lambda peer: sendbuf.at[1, peer, part], lambda owner: rbuf.at[owner * 2 + 1, part], ssem, rsem, HD + q * ND)
 
     for q in range(4):
         quarter(q).start()
@@ -336,7 +386,7 @@
         hids = [jnp.maximum(dot(xn, mtr_i[0]), 0.0).astype(BF) for xn in xns]
         y2s = [residual(y, dot(hid, mtr_o[0])) for y, hid in zip(ys, hids)]
         xns = [norm_lanes(y2.astype(F32)) for y2 in y2s]
-        abs_ = [dot_nt(opt[...], xn).astype(BF).astype(F32) * mrow for xn, mrow in zip(xns, mrows)]
+        abs_ = [dot_nt(opt[0], xn).astype(BF).astype(F32) * mrow for xn, mrow in zip(xns, mrows)]
         for r, y2, ab in zip(rs, y2s, abs_):
             m2_ref[r] = y2
             at_ref[r] = ab[0:HD].astype(BF)
@@ -351,20 +401,7 @@
 
     lax.fori_loop(0, 4, col_quarter, 0)
     for half in range(2):
-        bt_ref[:, :, RB * half:RB * half + RB] = scr[half, 0:512, :].astype(BF).reshape(HD, TI, RB)
-    for ex in [ex0] + [quarter(q) for q in range(4)]:
-        ex.wait_send()
-
-
-def pair_kernel(m2_ref, at_ref, bt_ref, z_ref, mt_ref, pm_ref, pt_ref,
-                opm_o, tmo_p, tmo_o, tmi_p, tmi_o, tas_w, tas_b, tas_o, tae_w, tae_b, tae_o, ptr_i, ptr_o,
-                mout_ref, zout_ref,
-                btall, obuf, opw, scr_a, scr_b, scr_x, a_c, ball1, ball2, gbuf, z1, zcol, sbias, ball3, bias_t,
-                wt, twt, zsend, z4, mrecv, mscr,
-                ch_s, ch_r, ds, dr):
-    me = lax.axis_index('dap')
-    group_barrier(me)
-    btall[me] = bt_ref[...]
+        btall[me, :, :, RB * half:RB * half + RB] = scr[half, 0:512, :].astype(BF).reshape(HD, TI, RB)
     ag0 = Chain(me, btall, ch_s.at[0], ch_r.at[0])
     ag0.start()
     scr_a[0:1024, :] = opm_o[0].astype(F32)
@@ -381,6 +418,10 @@
     inv_over = 1.0 / (1e-3 + dot_nt(mloc, mt_ref[...].astype(BF)))
     scr_x[0:TI, :] = inv_over
     ag0.finish()
+    ret = Return(me, lambda peer: m2_ref.at[:, pl.ds(pl.multiple_of(peer * HD, HD), HD), :], lambda owner: mrecv.at[owner], ms, mr)
+    ret.start(3, chip == 0)
+    ret.start(-3, chip == 3)
+    mrecv[me] = m2_ref[:, pl.ds(pl.multiple_of(me * HD, HD), HD), :]
 
     left = at_ref[...].reshape(512, SQ)
 
@@ -391,10 +432,6 @@
             obuf[:, pl.ds(pl.multiple_of(e * HD, HD), HD), :] = o
 
     tile_loop(HD, 2, opm_e)
-
-    ex_m = Direct(me, lambda peer: m2_ref.at[:, pl.ds(pl.multiple_of(peer * HD, HD), HD), :], lambda owner: mrecv.at[owner], ds, dr, 0)
-    mrecv[me] = m2_ref[:, pl.ds(pl.multiple_of(me * HD, HD), HD), :]
-    ex_m.start([1, 2])
 
     def opm_i(tiles):
         y_ts = [dot(opw[...], obuf[i]) * scr_x[pl.ds(i, 1), :] for i in tiles]
@@ -448,8 +485,17 @@
     front(tmo_p, z1, ball1, True)
     ag1 = Chain(me, ball1, ch_s.at[1], ch_r.at[1])
     ag1.start()
+    ret.start(1, chip == 0)
+    ret.start(-1, chip == 3)
+    ret.start_partner()
     a_c[...] = scr_a[...].astype(BF).reshape(RB, TI, RB)
-    ag1.finish()
+
+    def inner(t):
+        if t == 1:
+            ret.start(1, chip == 1)
+            ret.start(-1, chip == 2)
+
+    ag1.finish(inner)
 
     def out_c(cc, carry):
         for u in range(8):
@@ -458,10 +504,11 @@
         return carry
 
     lax.fori_loop(0, TI, out_c, 0)
-    ex_m.start([3, 4])
+    ret.start(1, chip == 2, (0,))
+    ret.start(-1, chip == 1, (0,))
     finish(tmo_o, z1, z1)
 
-    ex_z1 = Direct(me, lambda peer: z1.at[:, pl.ds(pl.multiple_of(peer * TI, TI), TI), :], lambda owner: zcol.at[0, owner], ds, dr, 8)
+    ex_z1 = Direct(me, lambda peer: z1.at[:, pl.ds(pl.multiple_of(peer * TI, TI), TI), :], lambda owner: zcol.at[0, owner], ssem, rsem, 64)
     ex_z1.start()
     zcol[0, me] = z1[:, pl.ds(pl.multiple_of(me * TI, TI), TI), :]
     front(tmi_p, z1, ball2, False)
@@ -481,7 +528,13 @@
 
     tile_loop(TI, 4, in_left)
     a_c[...] = scr_a[...].astype(BF).reshape(RB, TI, RB)
-    ag2.finish()
+
+    def two(t):
+        if t == 2:
+            ret.start(2, chip == 0)
+            ret.start(-2, chip == 3)
+
+    ag2.finish(two)
 
     def in_c(cc, carry):
         for u in range(8):
@@ -491,67 +544,71 @@
 
     lax.fori_loop(0, TI, in_c, 0)
     ex_z1.wait_send()
-    ex_m.start([5, 6, 7])
+    ret.start(1, chip == 2, (1,))
+    ret.start(-1, chip == 1, (1,))
     finish(tmi_o, z1, z1)
 
-    def tri_bias(w_ref, tile, slot, base):
-        wb_t = transpose_bf(jnp.concatenate([w_ref[0], jnp.zeros((RB, 124), BF)], 1))[0:8]
-
-        def body(tiles):
-            rows = [dot_nt(wb_t, norm_lanes(tile(i))) for i in tiles]
-            for i, row in zip(tiles, rows):
-                sbias[pl.ds(i, 8, stride=TI), :] = row
-
-        tile_loop(TI, 8, body)
+    def send_bias(slot, base):
         ball3[slot, me] = sbias[0:64, :].astype(BF).reshape(4, TI, RB)
-        ex = Direct(me, lambda peer: ball3.at[slot, me], lambda owner: ball3.at[slot, owner], ds, dr, base)
+        ex = Direct(me, lambda peer: ball3.at[slot, me], lambda owner: ball3.at[slot, owner], ssem, rsem, base)
         ex.start()
         return ex
 
-    def take_bias(slot):
-        for h in range(4):
-            bias_t[h] = ball3[slot, :, h].reshape(RB, RB).astype(F32).T * LOG2E
-
-    ex_s = tri_bias(tas_b, lambda i: z1[i].astype(F32), 0, TI)
-    prep_qkvg(tas_w, wt, RB)
+    def tas_bias(tiles):
+        rows = [dot_nt(tas_bt[0], norm_lanes(z1[i].astype(F32))) for i in tiles]
+        for i, row in zip(tiles, rows):
+            sbias[pl.ds(i, 4, stride=TI), :] = row
+
+    tile_loop(TI, 8, tas_bias)
+    ex_s = send_bias(0, 72)
+    prep_qkvg(tas_w, wt2, RB)
     ex_s.wait_recv()
-    take_bias(0)
+    for h in range(4):
+        bias_t[h] = ball3[0, :, h].reshape(RB, RB).astype(F32).T * LOG2E
+    ret.start(2, chip == 1, (0,))
+    ret.start(-2, chip == 2, (0,))
     tas_k = tas_w[0, :, RB:SQ]
 
     def tas_body(tiles):
         xs = [z1[i] for i in tiles]
         masks = [column_of(pm_ref[pl.ds(i, 1), :]) for i in tiles]
-        upds = attend_tiles([norm_lanes(x.astype(F32)) for x in xs], wt, tas_k, tas_o[0], 4, bias_t, masks, 4)
-        for i, x, upd in zip(tiles, xs, upds):
-            z1[i] = residual(x, upd)
+        upds = attend_tiles([norm_lanes(x.astype(F32)) for x in xs], wt2, tas_k, tas_o[0], 4, bias_t, masks, 4)
+        outs = [residual(x, upd) for x, upd in zip(xs, upds)]
+        rows = [dot_nt(tae_bt[0], norm_lanes(out.astype(F32))) for out in outs]
+        for i, out, row in zip(tiles, outs, rows):
+            z1[i] = out
+            sbias[pl.ds(i, 4, stride=TI), :] = row
 
     tile_loop(TI, 4, tas_body)
 
-    ex_z2 = Direct(me, lambda peer: z1.at[:, pl.ds(pl.multiple_of(peer * TI, TI), TI), :], lambda owner: zcol.at[1, owner], ds, dr, 24)
+    ex_z2 = Direct(me, lambda peer: z1.at[:, pl.ds(pl.multiple_of(peer * TI, TI), TI), :], lambda owner: zcol.at[1, owner], ssem, rsem, 80)
     ex_z2.start()
+    ex_e = send_bias(1, 88)
     zcol[1, me] = z1[:, pl.ds(pl.multiple_of(me * TI, TI), TI), :]
-    prep_qkvg(tae_w, wt, RB)
+    prep_qkvg(tae_w, wt2, RB)
     ex_z2.wait_recv()
     scr_b[...] = zcol[1].astype(F32).reshape(2048, RB)
-    ex_e = tri_bias(tae_b, lambda i: scr_b[pl.ds(i, RB, stride=TI), :], 1, HD)
     ex_e.wait_recv()
-    take_bias(1)
+    for h in range(4):
+        bias_t[h] = ball3[1, :, h].reshape(RB, RB).astype(F32) * LOG2E
+    ret.start(2, chip == 1, (1,))
+    ret.start(-2, chip == 2, (1,))
     tae_k = tae_w[0, :, RB:SQ]
 
     def tae_body(tiles):
         xs = [scr_b[pl.ds(i, RB, stride=TI), :] for i in tiles]
         masks = [column_of(pt_ref[pl.ds(me * TI + i, 1), :]) for i in tiles]
-        upds = attend_tiles([norm_lanes(x) for x in xs], wt, tae_k, tae_o[0], 4, bias_t, masks, 4)
+        upds = attend_tiles([norm_lanes(x) for x in xs], wt2, tae_k, tae_o[0], 4, bias_t, masks, 4)
         for i, x, upd in zip(tiles, xs, upds):
             scr_a[pl.ds(i, RB, stride=TI), :] = x + upd
 
     tile_loop(TI, 4, tae_body)
     zsend[...] = scr_a[...].astype(BF).reshape(8, TI, TI, RB)
-    ex_z3 = Direct(me, lambda peer: zsend.at[peer], lambda owner: z4.at[:, pl.ds(pl.multiple_of(owner * TI, TI), TI), :], ds, dr, 40)
+    ex_z3 = Direct(me, lambda peer: zsend.at[peer], lambda owner: z4.at[:, pl.ds(pl.multiple_of(owner * TI, TI), TI), :], ssem, rsem, 96)
     ex_z3.start()
     z4[:, pl.ds(pl.multiple_of(me * TI, TI), TI), :] = zsend[me]
 
-    ex_m.wait_recv()
+    ret.wait_recv()
 
     def widen(d, carry):
         for half in range(2):
@@ -578,7 +635,7 @@
             zout_ref[i] = out
 
     tile_loop(TI, 4, trans)
-    for ex in (ag0, ag1, ag2, ex_m, ex_s, ex_e, ex_z2, ex_z3):
+    for ex in [ex0] + [quarter(q) for q in range(4)] + [ag0, ag1, ag2, ret, ex_s, ex_e, ex_z2, ex_z3]:
         ex.wait_send()
 
 
@@ -586,88 +643,35 @@
     return pl.BlockSpec(shape, lambda g: (0,) * len(shape))
 
 
-def layer_of(shape, layer):
-    return pl.BlockSpec((1,) + shape[1:], lambda g: (layer,) + (0,) * (len(shape) - 1))
-
-
-def params(cid):
-    return pltpu.CompilerParams(collective_id=cid, has_side_effects=True, vmem_limit_bytes=VMEM_LIMIT)
-
-
-def run_masks(mm, pm):
-    outs = [(RB, SQ), (RB, RB)]
+def layer_of(shape):
+    return pl.BlockSpec((1,) + shape[1:], lambda g: (g,) + (0,) * (len(shape) - 1))
+
+
+def run(m, z, mm, pm, weights):
+    acts = (m, z, mm, pm)
+    outs = [(HD, RB, SQ), (TI, RB, RB)]
+    vm = pltpu.VMEM
     return pl.pallas_call(
-        mask_kernel,
-        grid=(1,),
-        out_shape=[jax.ShapeDtypeStruct(s, F32) for s in outs],
-        in_specs=[full(mm.shape), full(pm.shape)],
-        out_specs=[full(s) for s in outs],
-        scratch_shapes=[pltpu.VMEM((ND, HD, RB), F32), pltpu.VMEM((ND, TI, RB), F32),
-                        pltpu.SemaphoreType.DMA((TI,)), pltpu.SemaphoreType.DMA((TI,))],
-        compiler_params=params(0),
-    )(mm, pm)
-
-
-def run_msa(layer, m, z, rmask, mt, weights):
-    acts = (m, z, rmask, mt)
-    outs = [(TI, SQ, SQ), (TI, HD, SQ), (HD, TI, SQ)]
-    return pl.pallas_call(
-        msa_kernel,
-        grid=(1,),
+        blocks_kernel,
+        grid=(weights[0].shape[0],),
         out_shape=[jax.ShapeDtypeStruct(s, BF) for s in outs],
-        in_specs=[full(a.shape) for a in acts] + [layer_of(w.shape, layer) for w in weights],
+        in_specs=[full(a.shape) for a in acts] + [layer_of(w.shape) for w in weights],
         out_specs=[full(s) for s in outs],
         scratch_shapes=[
-            pltpu.VMEM((8, TI, RB), BF),
-            pltpu.VMEM((ND, 8, TI, RB), BF),
-            pltpu.VMEM((8, RB, RB), F32),
-            pltpu.VMEM((768, SQ), BF),
-            pltpu.VMEM((64, SQ), BF),
-            pltpu.VMEM((2, 2048, RB), F32),
-            pltpu.VMEM((2, ND, TI, TI, SQ), BF),
-            pltpu.VMEM((2 * ND, TI, TI, SQ), BF),
-            pltpu.VMEM((RB, RB), F32),
-            pltpu.SemaphoreType.DMA((48,)), pltpu.SemaphoreType.DMA((48,)),
+            vm((ND, HD, RB), F32), vm((ND, TI, RB), F32), vm((RB, SQ), F32), vm((RB, RB), F32), vm((HD, RB), F32), vm((TI, RB), F32),
+            vm((ND, 8, TI, RB), BF), vm((8, RB, RB), F32), vm((768, SQ), BF), vm((2, 2048, RB), F32),
+            vm((2, ND, TI, TI, SQ), BF), vm((2 * ND, TI, TI, SQ), BF), vm((RB, RB), F32), vm((TI, SQ, SQ), BF), vm((TI, HD, SQ), BF),
+            vm((ND, HD, TI, SQ), BF), vm((TI, 1024, RB), BF), vm((RB, 1024), BF),
+            vm((2048, RB), F32), vm((2048, RB), F32), vm((2048, RB), F32),
+            vm((RB, TI, RB), BF), vm((ND, RB, TI, RB), BF), vm((ND, RB, TI, RB), BF), vm((TI, RB, RB), F32), vm((TI, RB, RB), BF),
+            vm((2, ND, TI, TI, RB), BF), vm((RB, RB), F32), vm((2, ND, 4, TI, RB), BF),
+            vm((384, RB), BF), vm((512, RB), BF), vm((ND, TI, TI, RB), BF), vm((TI, RB, RB), BF),
+            vm((ND, TI, HD, SQ), BF), vm((2, 4096, RB), F32),
+            pltpu.SemaphoreType.DMA((120,)), pltpu.SemaphoreType.DMA((120,)),
+            pltpu.SemaphoreType.DMA((3, 2, 13)), pltpu.SemaphoreType.DMA((3, 2, 13)),
+            pltpu.SemaphoreType.DMA((14,)), pltpu.SemaphoreType.DMA((14,)),
         ],
-        compiler_params=params(1 + 2 * layer),
-    )(*acts, *weights)
-
-
-def run_pair(layer, m2, at, bt, z, mt, pm, pt, weights):
-    acts = (m2, at, bt, z, mt, pm, pt)
-    outs = [(HD, RB, SQ), (TI, RB, RB)]
-    return pl.pallas_call(
-        pair_kernel,
-        grid=(1,),
-        out_shape=[jax.ShapeDtypeStruct(s, BF) for s in outs],
-        in_specs=[full(a.shape) for a in acts] + [layer_of(w.shape, layer) for w in weights],
-        out_specs=[full(s) for s in outs],
-        scratch_shapes=[
-            pltpu.VMEM((ND, HD, TI, SQ), BF),
-            pltpu.VMEM((TI, 1024, RB), BF),
-            pltpu.VMEM((RB, 1024), BF),
-            pltpu.VMEM((2048, RB), F32),
-            pltpu.VMEM((2048, RB), F32),
-            pltpu.VMEM((2048, RB), F32),
-            pltpu.VMEM((RB, TI, RB), BF),
-            pltpu.VMEM((ND, RB, TI, RB), BF),
-            pltpu.VMEM((ND, RB, TI, RB), BF),
-            pltpu.VMEM((TI, RB, RB), F32),
-            pltpu.VMEM((TI, RB, RB), BF),
-            pltpu.VMEM((2, ND, TI, TI, RB), BF),
-            pltpu.VMEM((RB, RB), F32),
-            pltpu.VMEM((2, ND, 4, TI, RB), BF),
-            pltpu.VMEM((4, RB, RB), F32),
-            pltpu.VMEM((384, RB), BF),
-            pltpu.VMEM((512, RB), BF),
-            pltpu.VMEM((ND, TI, TI, RB), BF),
-            pltpu.VMEM((TI, RB, RB), BF),
-            pltpu.VMEM((ND, TI, HD, SQ), BF),
-            pltpu.VMEM((2, 4096, RB), F32),
-            pltpu.SemaphoreType.DMA((3, 13)), pltpu.SemaphoreType.DMA((3, 13)),
-            pltpu.SemaphoreType.DMA((48,)), pltpu.SemaphoreType.DMA((48,)),
-        ],
-        compiler_params=params(2 + 2 * layer),
+        compiler_params=pltpu.CompilerParams(collective_id=0, has_side_effects=True, vmem_limit_bytes=VMEM_LIMIT),
     )(*acts, *weights)
 
 
@@ -675,14 +679,8 @@
     row_spec = P(('req', 'dap'))
 
     def local_body(m, z, mm, pm, *weights):
-        (row_qkvg, row_bias, row_out, col_qkvg, col_out, mtr_in, mtr_out, opm_proj, opm_out) = weights[:9]
-        mt, pt = run_masks(mm, pm)
-        rmask = mm.astype(F32)
-        pmask = pm.astype(F32)
-        for layer in range(weights[0].shape[0]):
-            m2, at, bt = run_msa(layer, m, z, rmask, mt, (row_qkvg, row_bias, row_out, col_qkvg, col_out, mtr_in, mtr_out, opm_proj))
-            m, z = run_pair(layer, m2, at, bt, z, mt, pmask, pt, (opm_out,) + weights[9:])
-        return m, z
+        weights = [jnp.swapaxes(w, 1, 2) if k in (1, 7, 14, 17) else w for k, w in enumerate(weights)]
+        return tuple(run(m, z, mm, pm, weights))
 
     def run_blocks(*arrays):
         n_weights = len(arrays) - 4

time: 682 us -> 563 us (0.83)
  Pallas kernels: 668 us -> 558 us
    pallas_call x5 -> x1, Pallas kernels: 668 us -> 558 us  [run(): pl.pallas_call(blocks_kernel, grid=(weights[0].shape[0],), out_shape=[jax...]
where the time goes in v3:
time: 563 us
  Pallas kernels  558 us (99%)
    pallas_call x1, Pallas kernels, run(): pl.pallas_call(blocks_kernel, grid=(weights[0].shape[0],), out_shape=[jax...  558 us

profile of v3, /device:TPU:27, one launch (start us, length us, event | category | flops | bytes accessed | tf_op | source)
XLA Modules:
  0.0 562.9 jit_solution(3167982652739489674)
XLA Ops:
  0.6 558.3 %shard_map.248 = (bf16[32,128,256]{2,1,0:T(8,128)(2,1)}, bf16[16,128,128]{2,1,0:T(8,128)(2,1)}) custom-call(bf16[32,128,256]{2,1,0:T(8,128)(2,1)} %m_in.1, bf16[16,128,128]{2,1,0:T(8,128)(2,1)} %z_in.1, s32[32,128]{1,0:T(8,128)} %mm_ref.1, s32[16,128]{1,0:T(8,128)} %pm_in.1, bf16[2,256,1024]{2,1,0:T(8,128)(2,1)} %row_w.1, bf16[2,8,128]{2,1,0:T(8,128)(2,1)} %bitcast.5, ...), custom_call_target="tpu_custom_call" | custom-call | tf_op jit(solution)/shard_map/pallas_call | solution.py:654
  558.9 0.0 copy-start
  559.0 3.2 copy.29
  562.1 0.0 copy-done
  562.1 0.8 copy.30
Async XLA Ops:
  558.9 3.2 copy-start

commit v4 on v3

--- a/solution.py
+++ b/solution.py
@@ -158,6 +158,31 @@
                 def _():
                     self.cp(self.slot(t, True), self.me, 9 + t, half).wait_recv()
 
+    def stream(self, process, hook):
+        z = self.z
+
+        def take(t, other):
+            for sign, cond in ((-1, z >= t), (1, z + t <= 3)):
+                @pl.when(cond)
+                def _():
+                    if other:
+                        for half in range(2):
+                            self.cp(self.slot(sign * t, True), self.me, (6 if sign < 0 else 9) + t, half).wait_recv()
+                    process(self.slot(sign * t, other))
+
+        for t in range(1, 4):
+            for half in range(2):
+                self.forward(t, half, lambda c: c.wait_recv(), lambda c: c.start())
+            hook(t)
+            if t == 1:
+                for half in range(2):
+                    self.cp(self.partner, self.me, 6, half).wait_recv()
+                process(self.partner)
+            else:
+                take(t - 1, True)
+            take(t, False)
+        take(3, True)
+
     def wait_send(self):
         self.own(lambda c: c.wait_send())
         for t in range(1, 4):
@@ -281,14 +306,14 @@
                   mbuf, pbuf, mt_ref, pt_ref, rmask_ref, pm_ref,
                   ball, bias_t, wt, scr, sendbuf, rbuf, bscr, m2_ref, at_ref,
                   btall, obuf, opw, scr_a, scr_b, scr_x, a_c, ball1, ball2, gbuf, z1, zcol, sbias, ball3,
-                  wt2, twt, zsend, z4, mrecv, mscr,
+                  wt2, twt, twt2, zall, zsend, z4, mrecv, mscr,
                   ssem, rsem, ch_s, ch_r, ms, mr):
     me = lax.axis_index('dap')
     chip = lax.div(me, 2)
     first = pl.program_id(0) == 0
     group_barrier(me)
     ex_k = [Direct(me, lambda peer, buf=buf: buf.at[me], lambda owner, buf=buf: buf.at[owner], ssem, rsem, base)
-            for buf, base in ((mbuf, 104), (pbuf, 112))]
+            for buf, base in ((mbuf, 0), (pbuf, 8))]
 
     @pl.when(first)
     def _():
@@ -360,10 +385,10 @@
             ex0.start()
 
     def quarter(q):
-        part = pl.ds(pl.multiple_of(q * 4, 4), 4)
+        part = pl.ds(q * 2, 2)
         return Direct(me, lambda peer: sendbuf.at[1, peer, part], lambda owner: rbuf.at[owner * 2 + 1, part], ssem, rsem, HD + q * ND)
 
-    for q in range(4):
+    for q in range(8):
         quarter(q).start()
     ex_b.wait_send()
     prep_qkvg(col_w, wt, SQ)
@@ -395,11 +420,11 @@
 
     def col_quarter(q, carry):
         quarter(q).wait_recv()
-        tile_loop(4, 1, lambda rs: col_body([q * 4 + r for r in rs]))
-        tile_loop(4, 2, lambda rs: mtr_body([q * 4 + r for r in rs]))
+        tile_loop(2, 1, lambda rs: col_body([q * 2 + r for r in rs]))
+        mtr_body([q * 2, q * 2 + 1])
         return carry
 
-    lax.fori_loop(0, 4, col_quarter, 0)
+    lax.fori_loop(0, 8, col_quarter, 0)
     for half in range(2):
         btall[me, :, :, RB * half:RB * half + RB] = scr[half, 0:512, :].astype(BF).reshape(HD, TI, RB)
     ag0 = Chain(me, btall, ch_s.at[0], ch_r.at[0])
@@ -417,6 +442,7 @@
     mloc = mt_ref[pl.ds(pl.multiple_of(me * TI, TI), TI), :].astype(BF)
     inv_over = 1.0 / (1e-3 + dot_nt(mloc, mt_ref[...].astype(BF)))
     scr_x[0:TI, :] = inv_over
+    twt[...] = transpose_bf(tmo_p[0, :, 0:512])
     ag0.finish()
     ret = Return(me, lambda peer: m2_ref.at[:, pl.ds(pl.multiple_of(peer * HD, HD), HD), :], lambda owner: mrecv.at[owner], ms, mr)
     ret.start(3, chip == 0)
@@ -441,9 +467,7 @@
 
     tile_loop(TI, 4, opm_i)
 
-    def front(w_ref, z_src, ball, left_too):
-        wt_l = twt
-        wt_l[...] = transpose_bf(w_ref[0, :, 0:512])
+    def front(w_ref, wt_l, z_src, ball, left_too):
         wg = w_ref[0, :, 512:640]
 
         def body(tiles):
@@ -482,7 +506,7 @@
 
         tile_loop(TI, 4, body)
 
-    front(tmo_p, z1, ball1, True)
+    front(tmo_p, twt, z1, ball1, True)
     ag1 = Chain(me, ball1, ch_s.at[1], ch_r.at[1])
     ag1.start()
     ret.start(1, chip == 0)
@@ -490,6 +514,8 @@
     ret.start_partner()
     a_c[...] = scr_a[...].astype(BF).reshape(RB, TI, RB)
 
+    twt2[...] = transpose_bf(tmi_p[0, :, 0:512])
+
     def inner(t):
         if t == 1:
             ret.start(1, chip == 1)
@@ -508,33 +534,44 @@
     ret.start(-1, chip == 1, (0,))
     finish(tmo_o, z1, z1)
 
-    ex_z1 = Direct(me, lambda peer: z1.at[:, pl.ds(pl.multiple_of(peer * TI, TI), TI), :], lambda owner: zcol.at[0, owner], ssem, rsem, 64)
-    ex_z1.start()
-    zcol[0, me] = z1[:, pl.ds(pl.multiple_of(me * TI, TI), TI), :]
-    front(tmi_p, z1, ball2, False)
-    ag2 = Chain(me, ball2, ch_s.at[2], ch_r.at[2])
+    zall[me] = z1[...]
+    ag2 = Chain(me, zall, ch_s.at[2], ch_r.at[2])
     ag2.start()
-    ex_z1.wait_recv()
-    scr_b[...] = zcol[0].astype(F32).reshape(2048, RB)
-
-    def in_left(tiles):
-        xns = [norm_lanes(scr_b[pl.ds(i, RB, stride=TI), :]) for i in tiles]
-        mrows = [pt_ref[pl.ds(me * TI + i, 1), :] for i in tiles]
-        pas = [dot_nt(twt[0:RB, :], xn) for xn in xns]
-        pgs = [dot_nt(twt[SQ:384, :], xn) for xn in xns]
-        lefts = [mrow * jax.nn.sigmoid(pg) * pa for mrow, pg, pa in zip(mrows, pgs, pas)]
-        for i, left in zip(tiles, lefts):
-            scr_a[pl.ds(i, RB, stride=TI), :] = left
-
-    tile_loop(TI, 4, in_left)
-    a_c[...] = scr_a[...].astype(BF).reshape(RB, TI, RB)
+    front(tmi_p, twt2, z1, ball2, False)
+    prep_qkvg(tas_w, wt2, RB)
+
+    def in_right(slot):
+        def body(tiles):
+            xns = [norm_lanes(zall[slot, i].astype(F32)) for i in tiles]
+            mrows = [pbuf[slot, pl.ds(i, 1), :] for i in tiles]
+            pbs = [dot_nt(twt2[RB:SQ, :], xn) for xn in xns]
+            pgs = [dot_nt(twt2[384:512, :], xn) for xn in xns]
+            rights = [mrow * jax.nn.sigmoid(pg) * pb for mrow, pg, pb in zip(mrows, pgs, pbs)]
+            for i, right in zip(tiles, rights):
+                scr_b[pl.ds(i, RB, stride=TI), :] = right
+
+        tile_loop(TI, 4, body)
+        ball2[slot] = scr_b[...].astype(BF).reshape(RB, TI, RB)
 
     def two(t):
         if t == 2:
             ret.start(2, chip == 0)
             ret.start(-2, chip == 3)
 
-    ag2.finish(two)
+    ag2.stream(in_right, two)
+    scr_b[...] = zall[:, :, pl.ds(pl.multiple_of(me * TI, TI), TI), :].astype(F32).reshape(2048, RB)
+
+    def in_left(tiles):
+        xns = [norm_lanes(scr_b[pl.ds(i, RB, stride=TI), :]) for i in tiles]
+        mrows = [pt_ref[pl.ds(me * TI + i, 1), :] for i in tiles]
+        pas = [dot_nt(twt2[0:RB, :], xn) for xn in xns]
+        pgs = [dot_nt(twt2[SQ:384, :], xn) for xn in xns]
+        lefts = [mrow * jax.nn.sigmoid(pg) * pa for mrow, pg, pa in zip(mrows, pgs, pas)]
+        for i, left in zip(tiles, lefts):
+            scr_a[pl.ds(i, RB, stride=TI), :] = left
+
+    tile_loop(TI, 4, in_left)
+    a_c[...] = scr_a[...].astype(BF).reshape(RB, TI, RB)
 
     def in_c(cc, carry):
         for u in range(8):
@@ -543,7 +580,6 @@
         return carry
 
     lax.fori_loop(0, TI, in_c, 0)
-    ex_z1.wait_send()
     ret.start(1, chip == 2, (1,))
     ret.start(-1, chip == 1, (1,))
     finish(tmi_o, z1, z1)
@@ -560,8 +596,7 @@
             sbias[pl.ds(i, 4, stride=TI), :] = row
 
     tile_loop(TI, 8, tas_bias)
-    ex_s = send_bias(0, 72)
-    prep_qkvg(tas_w, wt2, RB)
+    ex_s = send_bias(0, 96)
     ex_s.wait_recv()
     for h in range(4):
         bias_t[h] = ball3[0, :, h].reshape(RB, RB).astype(F32).T * LOG2E
@@ -581,13 +616,13 @@
 
     tile_loop(TI, 4, tas_body)
 
-    ex_z2 = Direct(me, lambda peer: z1.at[:, pl.ds(pl.multiple_of(peer * TI, TI), TI), :], lambda owner: zcol.at[1, owner], ssem, rsem, 80)
+    ex_z2 = Direct(me, lambda peer: z1.at[:, pl.ds(pl.multiple_of(peer * TI, TI), TI), :], lambda owner: zcol.at[owner], ssem, rsem, 104)
     ex_z2.start()
-    ex_e = send_bias(1, 88)
-    zcol[1, me] = z1[:, pl.ds(pl.multiple_of(me * TI, TI), TI), :]
+    ex_e = send_bias(1, 112)
+    zcol[me] = z1[:, pl.ds(pl.multiple_of(me * TI, TI), TI), :]
     prep_qkvg(tae_w, wt2, RB)
     ex_z2.wait_recv()
-    scr_b[...] = zcol[1].astype(F32).reshape(2048, RB)
+    scr_b[...] = zcol[...].astype(F32).reshape(2048, RB)
     ex_e.wait_recv()
     for h in range(4):
         bias_t[h] = ball3[1, :, h].reshape(RB, RB).astype(F32) * LOG2E
@@ -604,7 +639,7 @@
 
     tile_loop(TI, 4, tae_body)
     zsend[...] = scr_a[...].astype(BF).reshape(8, TI, TI, RB)
-    ex_z3 = Direct(me, lambda peer: zsend.at[peer], lambda owner: z4.at[:, pl.ds(pl.multiple_of(owner * TI, TI), TI), :], ssem, rsem, 96)
+    ex_z3 = Direct(me, lambda peer: zsend.at[peer], lambda owner: z4.at[:, pl.ds(pl.multiple_of(owner * TI, TI), TI), :], ssem, rsem, 120)
     ex_z3.start()
     z4[:, pl.ds(pl.multiple_of(me * TI, TI), TI), :] = zsend[me]
 
@@ -635,7 +670,7 @@
             zout_ref[i] = out
 
     tile_loop(TI, 4, trans)
-    for ex in [ex0] + [quarter(q) for q in range(4)] + [ag0, ag1, ag2, ret, ex_s, ex_e, ex_z2, ex_z3]:
+    for ex in [ex0] + [quarter(q) for q in range(8)] + [ag0, ag1, ag2, ret, ex_s, ex_e, ex_z2, ex_z3]:
         ex.wait_send()
 
 
@@ -664,10 +699,10 @@
             vm((ND, HD, TI, SQ), BF), vm((TI, 1024, RB), BF), vm((RB, 1024), BF),
             vm((2048, RB), F32), vm((2048, RB), F32), vm((2048, RB), F32),
             vm((RB, TI, RB), BF), vm((ND, RB, TI, RB), BF), vm((ND, RB, TI, RB), BF), vm((TI, RB, RB), F32), vm((TI, RB, RB), BF),
-            vm((2, ND, TI, TI, RB), BF), vm((RB, RB), F32), vm((2, ND, 4, TI, RB), BF),
-            vm((384, RB), BF), vm((512, RB), BF), vm((ND, TI, TI, RB), BF), vm((TI, RB, RB), BF),
+            vm((ND, TI, TI, RB), BF), vm((RB, RB), F32), vm((2, ND, 4, TI, RB), BF),
+            vm((384, RB), BF), vm((512, RB), BF), vm((512, RB), BF), vm((ND, TI, RB, RB), BF), vm((ND, TI, TI, RB), BF), vm((TI, RB, RB), BF),
             vm((ND, TI, HD, SQ), BF), vm((2, 4096, RB), F32),
-            pltpu.SemaphoreType.DMA((120,)), pltpu.SemaphoreType.DMA((120,)),
+            pltpu.SemaphoreType.DMA((RB,)), pltpu.SemaphoreType.DMA((RB,)),
             pltpu.SemaphoreType.DMA((3, 2, 13)), pltpu.SemaphoreType.DMA((3, 2, 13)),
             pltpu.SemaphoreType.DMA((14,)), pltpu.SemaphoreType.DMA((14,)),
         ],

time: 563 us -> 559 us (level)
  no operation moved by 1% of the time
where the time goes in v4:
time: 559 us
  Pallas kernels  554 us (99%)
    pallas_call x1, Pallas kernels, run(): pl.pallas_call(blocks_kernel, grid=(weights[0].shape[0],), out_shape=[jax...  554 us

profile of v4, /device:TPU:27, one launch (start us, length us, event | category | flops | bytes accessed | tf_op | source)
XLA Modules:
  0.0 559.0 jit_solution(1151285863080174061)
XLA Ops:
  0.6 554.4 %shard_map.248 = (bf16[32,128,256]{2,1,0:T(8,128)(2,1)}, bf16[16,128,128]{2,1,0:T(8,128)(2,1)}) custom-call(bf16[32,128,256]{2,1,0:T(8,128)(2,1)} %m_in.1, bf16[16,128,128]{2,1,0:T(8,128)(2,1)} %z_in.1, s32[32,128]{1,0:T(8,128)} %mm_ref.1, s32[16,128]{1,0:T(8,128)} %pm_in.1, bf16[2,256,1024]{2,1,0:T(8,128)(2,1)} %row_w.1, bf16[2,8,128]{2,1,0:T(8,128)(2,1)} %bitcast.5, ...), custom_call_target="tpu_custom_call" | custom-call | tf_op jit(solution)/shard_map/pallas_call | solution.py:689
  555.0 0.0 copy-start
  555.0 3.2 copy.29
  558.2 0.0 copy-done
  558.2 0.8 copy.30
Async XLA Ops:
  555.0 3.2 copy-start

commit v5 on v4

--- a/solution.py
+++ b/solution.py
@@ -16,6 +16,7 @@
 SQ = 256
 TI = 16
 HD = 32
+EARLY = 3
 
 
 def dot(a, b):
@@ -162,13 +163,19 @@
         z = self.z
 
         def take(t, other):
-            for sign, cond in ((-1, z >= t), (1, z + t <= 3)):
-                @pl.when(cond)
+            def one(k, carry):
+                off = (2 * k - 1) * t
+
+                @pl.when(jnp.logical_and(z + off >= 0, z + off <= 3))
                 def _():
                     if other:
                         for half in range(2):
-                            self.cp(self.slot(sign * t, True), self.me, (6 if sign < 0 else 9) + t, half).wait_recv()
-                    process(self.slot(sign * t, other))
+                            self.cp(self.slot(off, True), self.me, 6 + 3 * k + t, half).wait_recv()
+                    process(self.slot(off, other))
+
+                return carry
+
+            lax.fori_loop(0, 2, one, 0)
 
         for t in range(1, 4):
             for half in range(2):
@@ -359,7 +366,11 @@
         bias_t[h] = ball[:, h].reshape(RB, RB).astype(F32).T * LOG2E
     row_k = row_w[0, :, SQ:512]
     row_ow = row_o[0]
-    for ck in range(2):
+    def piece(ck, q):
+        part = pl.ds(q * 2, 2)
+        return Direct(me, lambda peer: sendbuf.at[ck, peer, part], lambda owner: rbuf.at[owner * 2 + ck, part], ssem, rsem, 24 + ck * 64 + q * ND)
+
+    def half_rows(ck, carry):
         def row_body(sls):
             xs = [m_ref[ck * TI + sl] for sl in sls]
             masks = [column_of(rmask_ref[pl.ds(ck * TI + sl, 1), :]) for sl in sls]
@@ -370,7 +381,7 @@
                 for half in range(2):
                     scr[half, pl.ds(sl, RB, stride=TI), :] = y[:, RB * half:RB * half + RB]
 
-        tile_loop(TI, 2, row_body)
+        tile_loop(TI, 8, row_body)
 
         def pack(d, carry):
             for half in range(2):
@@ -380,19 +391,20 @@
 
         lax.fori_loop(0, 8, pack, 0)
         rbuf[me * 2 + ck] = sendbuf[ck, me]
-        if ck == 0:
-            ex0 = Direct(me, lambda peer: sendbuf.at[0, peer], lambda owner: rbuf.at[owner * 2], ssem, rsem, 24)
-            ex0.start()
-
-    def quarter(q):
-        part = pl.ds(q * 2, 2)
-        return Direct(me, lambda peer: sendbuf.at[1, peer, part], lambda owner: rbuf.at[owner * 2 + 1, part], ssem, rsem, HD + q * ND)
-
-    for q in range(8):
-        quarter(q).start()
+        for q in range(EARLY):
+            piece(ck, q).start()
+        return carry
+
+    lax.fori_loop(0, 2, half_rows, 0)
+
+    def send_rest(q, carry):
+        piece(0, q).start()
+        piece(1, q).start()
+        return carry
+
+    lax.fori_loop(EARLY, 8, send_rest, 0)
     ex_b.wait_send()
     prep_qkvg(col_w, wt, SQ)
-    ex0.wait_recv()
     col_k = col_w[0, :, SQ:512]
     col_ow = col_o[0]
 
@@ -400,7 +412,7 @@
         xs = [rbuf[:, r].reshape(SQ, SQ) for r in rs]
         mrows = [mt_ref[pl.ds(me * TI + r, 1), :] for r in rs]
         masks = [column_of(mrow) for mrow in mrows]
-        upds = attend_tiles([norm_lanes(x.astype(F32)) for x in xs], wt, col_k, col_ow, 8, None, masks, 2)
+        upds = attend_tiles([norm_lanes(x.astype(F32)) for x in xs], wt, col_k, col_ow, 8, None, masks, 4)
         for r, x, upd in zip(rs, xs, upds):
             m2_ref[r] = residual(x, upd)
 
@@ -419,8 +431,9 @@
                 scr[half, pl.ds(r, HD, stride=TI), :] = ab[HD:2 * HD, RB * half:RB * half + RB]
 
     def col_quarter(q, carry):
-        quarter(q).wait_recv()
-        tile_loop(2, 1, lambda rs: col_body([q * 2 + r for r in rs]))
+        piece(0, q).wait_recv()
+        piece(1, q).wait_recv()
+        col_body([q * 2, q * 2 + 1])
         mtr_body([q * 2, q * 2 + 1])
         return carry
 
@@ -457,7 +470,7 @@
         for e, o in zip(es, os_):
             obuf[:, pl.ds(pl.multiple_of(e * HD, HD), HD), :] = o
 
-    tile_loop(HD, 2, opm_e)
+    tile_loop(HD, 4, opm_e)
 
     def opm_i(tiles):
         y_ts = [dot(opw[...], obuf[i]) * scr_x[pl.ds(i, 1), :] for i in tiles]
@@ -465,7 +478,7 @@
         for i, out in zip(tiles, outs):
             z1[i] = out
 
-    tile_loop(TI, 4, opm_i)
+    tile_loop(TI, 8, opm_i)
 
     def front(w_ref, wt_l, z_src, ball, left_too):
         wg = w_ref[0, :, 512:640]
@@ -491,7 +504,7 @@
                 scr_b[pl.ds(i, RB, stride=TI), :] = right
                 gbuf[i] = gate
 
-        tile_loop(TI, 4, body)
+        tile_loop(TI, 8, body)
         ball[me] = scr_b[...].astype(BF).reshape(RB, TI, RB)
 
     def finish(w_ref, z_src, z_dst):
@@ -504,7 +517,7 @@
             for i, out in zip(tiles, outs):
                 z_dst[i] = out
 
-        tile_loop(TI, 4, body)
+        tile_loop(TI, 8, body)
 
     front(tmo_p, twt, z1, ball1, True)
     ag1 = Chain(me, ball1, ch_s.at[1], ch_r.at[1])
@@ -550,7 +563,7 @@
             for i, right in zip(tiles, rights):
                 scr_b[pl.ds(i, RB, stride=TI), :] = right
 
-        tile_loop(TI, 4, body)
+        tile_loop(TI, 8, body)
         ball2[slot] = scr_b[...].astype(BF).reshape(RB, TI, RB)
 
     def two(t):
@@ -570,7 +583,7 @@
         for i, left in zip(tiles, lefts):
             scr_a[pl.ds(i, RB, stride=TI), :] = left
 
-    tile_loop(TI, 4, in_left)
+    tile_loop(TI, 8, in_left)
     a_c[...] = scr_a[...].astype(BF).reshape(RB, TI, RB)
 
     def in_c(cc, carry):
@@ -596,7 +609,7 @@
             sbias[pl.ds(i, 4, stride=TI), :] = row
 
     tile_loop(TI, 8, tas_bias)
-    ex_s = send_bias(0, 96)
+    ex_s = send_bias(0, 152)
     ex_s.wait_recv()
     for h in range(4):
         bias_t[h] = ball3[0, :, h].reshape(RB, RB).astype(F32).T * LOG2E
@@ -614,11 +627,11 @@
             z1[i] = out
             sbias[pl.ds(i, 4, stride=TI), :] = row
 
-    tile_loop(TI, 4, tas_body)
-
-    ex_z2 = Direct(me, lambda peer: z1.at[:, pl.ds(pl.multiple_of(peer * TI, TI), TI), :], lambda owner: zcol.at[owner], ssem, rsem, 104)
+    tile_loop(TI, 8, tas_body)
+
+    ex_z2 = Direct(me, lambda peer: z1.at[:, pl.ds(pl.multiple_of(peer * TI, TI), TI), :], lambda owner: zcol.at[owner], ssem, rsem, 160)
     ex_z2.start()
-    ex_e = send_bias(1, 112)
+    ex_e = send_bias(1, 168)
     zcol[me] = z1[:, pl.ds(pl.multiple_of(me * TI, TI), TI), :]
     prep_qkvg(tae_w, wt2, RB)
     ex_z2.wait_recv()
@@ -637,9 +650,9 @@
         for i, x, upd in zip(tiles, xs, upds):
             scr_a[pl.ds(i, RB, stride=TI), :] = x + upd
 
-    tile_loop(TI, 4, tae_body)
+    tile_loop(TI, 8, tae_body)
     zsend[...] = scr_a[...].astype(BF).reshape(8, TI, TI, RB)
-    ex_z3 = Direct(me, lambda peer: zsend.at[peer], lambda owner: z4.at[:, pl.ds(pl.multiple_of(owner * TI, TI), TI), :], ssem, rsem, 120)
+    ex_z3 = Direct(me, lambda peer: zsend.at[peer], lambda owner: z4.at[:, pl.ds(pl.multiple_of(owner * TI, TI), TI), :], ssem, rsem, 176)
     ex_z3.start()
     z4[:, pl.ds(pl.multiple_of(me * TI, TI), TI), :] = zsend[me]
 
@@ -669,8 +682,14 @@
         for i, out in zip(tiles, outs):
             zout_ref[i] = out
 
-    tile_loop(TI, 4, trans)
-    for ex in [ex0] + [quarter(q) for q in range(8)] + [ag0, ag1, ag2, ret, ex_s, ex_e, ex_z2, ex_z3]:
+    tile_loop(TI, 8, trans)
+    def sent(q, carry):
+        piece(0, q).wait_send()
+        piece(1, q).wait_send()
+        return carry
+
+    lax.fori_loop(0, 8, sent, 0)
+    for ex in (ag0, ag1, ag2, ret, ex_s, ex_e, ex_z2, ex_z3):
         ex.wait_send()
 
 
@@ -702,7 +721,7 @@
             vm((ND, TI, TI, RB), BF), vm((RB, RB), F32), vm((2, ND, 4, TI, RB), BF),
             vm((384, RB), BF), vm((512, RB), BF), vm((512, RB), BF), vm((ND, TI, RB, RB), BF), vm((ND, TI, TI, RB), BF), vm((TI, RB, RB), BF),
             vm((ND, TI, HD, SQ), BF), vm((2, 4096, RB), F32),
-            pltpu.SemaphoreType.DMA((RB,)), pltpu.SemaphoreType.DMA((RB,)),
+            pltpu.SemaphoreType.DMA((184,)), pltpu.SemaphoreType.DMA((184,)),
             pltpu.SemaphoreType.DMA((3, 2, 13)), pltpu.SemaphoreType.DMA((3, 2, 13)),
             pltpu.SemaphoreType.DMA((14,)), pltpu.SemaphoreType.DMA((14,)),
         ],

time: 559 us -> 494 us (0.88)
  Pallas kernels: 554 us -> 489 us
    pallas_call x1, Pallas kernels: 554 us -> 489 us  [run(): pl.pallas_call(blocks_kernel, grid=(weights[0].shape[0],), out_shape=[jax...]
where the time goes in v5:
time: 494 us
  Pallas kernels  489 us (99%)
    pallas_call x1, Pallas kernels, run(): pl.pallas_call(blocks_kernel, grid=(weights[0].shape[0],), out_shape=[jax...  489 us

profile of v5, /device:TPU:27, one launch (start us, length us, event | category | flops | bytes accessed | tf_op | source)
XLA Modules:
  0.0 493.7 jit_solution(17577538352570929554)
XLA Ops:
  0.6 489.0 %shard_map.248 = (bf16[32,128,256]{2,1,0:T(8,128)(2,1)}, bf16[16,128,128]{2,1,0:T(8,128)(2,1)}) custom-call(bf16[32,128,256]{2,1,0:T(8,128)(2,1)} %m_in.1, bf16[16,128,128]{2,1,0:T(8,128)(2,1)} %z_in.1, s32[32,128]{1,0:T(8,128)} %mm_ref.1, s32[16,128]{1,0:T(8,128)} %pm_in.1, bf16[2,256,1024]{2,1,0:T(8,128)(2,1)} %row_w.1, bf16[2,8,128]{2,1,0:T(8,128)(2,1)} %bitcast.5, ...), custom_call_target="tpu_custom_call" | custom-call | tf_op jit(solution)/shard_map/pallas_call | solution.py:708
  489.7 0.0 copy-start
  489.7 3.2 copy.29
  492.9 0.0 copy-done
  492.9 0.8 copy.30
Async XLA Ops:
  489.7 3.2 copy-start

commit v6 on v5

--- a/solution.py
+++ b/solution.py
@@ -331,11 +331,6 @@
         for ex in ex_k:
             ex.start()
 
-        def take(s, carry):
-            mout_ref[s] = m_in[s]
-            return carry
-
-        lax.fori_loop(0, HD, take, 0)
         zout_ref[...] = z_in[...]
 
     m_ref, z_ref = mout_ref, zout_ref
@@ -350,6 +345,15 @@
     ball[me] = bscr[...].astype(BF).reshape(8, TI, RB)
     ex_b = Direct(me, lambda peer: ball.at[me], lambda owner: ball.at[owner], ssem, rsem, TI)
     ex_b.start()
+
+    @pl.when(first)
+    def _():
+        def take(s, carry):
+            mout_ref[s] = m_in[s]
+            return carry
+
+        lax.fori_loop(0, HD, take, 0)
+
     prep_qkvg(row_w, wt, SQ)
 
     @pl.when(first)
@@ -375,7 +379,7 @@
             xs = [m_ref[ck * TI + sl] for sl in sls]
             masks = [column_of(rmask_ref[pl.ds(ck * TI + sl, 1), :]) for sl in sls]
             xns = [norm_lanes(x.astype(F32)) for x in xs]
-            upds = attend_tiles(xns, wt, row_k, row_ow, 8, bias_t, masks, 4)
+            upds = attend_tiles(xns, wt, row_k, row_ow, 8, bias_t, masks, 6)
             for sl, x, upd in zip(sls, xs, upds):
                 y = residual(x, upd).astype(F32)
                 for half in range(2):
@@ -412,7 +416,7 @@
         xs = [rbuf[:, r].reshape(SQ, SQ) for r in rs]
         mrows = [mt_ref[pl.ds(me * TI + r, 1), :] for r in rs]
         masks = [column_of(mrow) for mrow in mrows]
-        upds = attend_tiles([norm_lanes(x.astype(F32)) for x in xs], wt, col_k, col_ow, 8, None, masks, 4)
+        upds = attend_tiles([norm_lanes(x.astype(F32)) for x in xs], wt, col_k, col_ow, 8, None, masks, 6)
         for r, x, upd in zip(rs, xs, upds):
             m2_ref[r] = residual(x, upd)
 
@@ -470,7 +474,7 @@
         for e, o in zip(es, os_):
             obuf[:, pl.ds(pl.multiple_of(e * HD, HD), HD), :] = o
 
-    tile_loop(HD, 4, opm_e)
+    tile_loop(HD, 8, opm_e)
 
     def opm_i(tiles):
         y_ts = [dot(opw[...], obuf[i]) * scr_x[pl.ds(i, 1), :] for i in tiles]
@@ -537,12 +541,12 @@
     ag1.finish(inner)
 
     def out_c(cc, carry):
-        for u in range(8):
-            c = cc * 8 + u
+        for u in range(TI):
+            c = cc * TI + u
             scr_x[pl.ds(pl.multiple_of(c * TI, TI), TI), :] = dot_nt(a_c[c], ball1[:, c].reshape(RB, RB))
         return carry
 
-    lax.fori_loop(0, TI, out_c, 0)
+    lax.fori_loop(0, 8, out_c, 0)
     ret.start(1, chip == 2, (0,))
     ret.start(-1, chip == 1, (0,))
     finish(tmo_o, z1, z1)
@@ -587,12 +591,12 @@
     a_c[...] = scr_a[...].astype(BF).reshape(RB, TI, RB)
 
     def in_c(cc, carry):
-        for u in range(8):
-            c = cc * 8 + u
+        for u in range(TI):
+            c = cc * TI + u
             scr_x[pl.ds(pl.multiple_of(c * TI, TI), TI), :] = dot(a_c[c], ball2[:, c].reshape(RB, RB))
         return carry
 
-    lax.fori_loop(0, TI, in_c, 0)
+    lax.fori_loop(0, 8, in_c, 0)
     ret.start(1, chip == 2, (1,))
     ret.start(-1, chip == 1, (1,))
     finish(tmi_o, z1, z1)
@@ -609,7 +613,7 @@
             sbias[pl.ds(i, 4, stride=TI), :] = row
 
     tile_loop(TI, 8, tas_bias)
-    ex_s = send_bias(0, 152)
+    ex_s = send_bias(0, 168)
     ex_s.wait_recv()
     for h in range(4):
         bias_t[h] = ball3[0, :, h].reshape(RB, RB).astype(F32).T * LOG2E
@@ -626,15 +630,20 @@
         for i, out, row in zip(tiles, outs, rows):
             z1[i] = out
             sbias[pl.ds(i, 4, stride=TI), :] = row
+        half_z(tiles[0]).start()
+
+    def half_z(row):
+        rows = pl.ds(pl.multiple_of(row, 8), 8)
+        return Direct(me, lambda peer: z1.at[rows, pl.ds(pl.multiple_of(peer * TI, TI), TI), :], lambda owner: zcol.at[owner, rows],
+                      ssem, rsem, 152 + row)
 
     tile_loop(TI, 8, tas_body)
 
-    ex_z2 = Direct(me, lambda peer: z1.at[:, pl.ds(pl.multiple_of(peer * TI, TI), TI), :], lambda owner: zcol.at[owner], ssem, rsem, 160)
-    ex_z2.start()
-    ex_e = send_bias(1, 168)
+    ex_e = send_bias(1, 184)
     zcol[me] = z1[:, pl.ds(pl.multiple_of(me * TI, TI), TI), :]
     prep_qkvg(tae_w, wt2, RB)
-    ex_z2.wait_recv()
+    for row in (0, 8):
+        half_z(row).wait_recv()
     scr_b[...] = zcol[...].astype(F32).reshape(2048, RB)
     ex_e.wait_recv()
     for h in range(4):
@@ -689,7 +698,7 @@
         return carry
 
     lax.fori_loop(0, 8, sent, 0)
-    for ex in (ag0, ag1, ag2, ret, ex_s, ex_e, ex_z2, ex_z3):
+    for ex in (ag0, ag1, ag2, ret, ex_s, ex_e, half_z(0), half_z(8), ex_z3):
         ex.wait_send()
 
 
@@ -721,7 +730,7 @@
             vm((ND, TI, TI, RB), BF), vm((RB, RB), F32), vm((2, ND, 4, TI, RB), BF),
             vm((384, RB), BF), vm((512, RB), BF), vm((512, RB), BF), vm((ND, TI, RB, RB), BF), vm((ND, TI, TI, RB), BF), vm((TI, RB, RB), BF),
             vm((ND, TI, HD, SQ), BF), vm((2, 4096, RB), F32),
-            pltpu.SemaphoreType.DMA((184,)), pltpu.SemaphoreType.DMA((184,)),
+            pltpu.SemaphoreType.DMA((192,)), pltpu.SemaphoreType.DMA((192,)),
             pltpu.SemaphoreType.DMA((3, 2, 13)), pltpu.SemaphoreType.DMA((3, 2, 13)),
             pltpu.SemaphoreType.DMA((14,)), pltpu.SemaphoreType.DMA((14,)),
         ],

time: 494 us -> 491 us (level)
  no operation moved by 1% of the time
where the time goes in v6:
time: 491 us; the launch traced here: 490 us
  Pallas kernels  486 us (99%)
    pallas_call x1, Pallas kernels, run(): pl.pallas_call(blocks_kernel, grid=(weights[0].shape[0],), out_shape=[jax...  486 us

profile of v6, /device:TPU:27, one launch (start us, length us, event | category | flops | bytes accessed | tf_op | source)
XLA Modules:
  0.0 490.4 jit_solution(15961835648034741428)
XLA Ops:
  0.6 485.7 %shard_map.248 = (bf16[32,128,256]{2,1,0:T(8,128)(2,1)}, bf16[16,128,128]{2,1,0:T(8,128)(2,1)}) custom-call(bf16[32,128,256]{2,1,0:T(8,128)(2,1)} %m_in.1, bf16[16,128,128]{2,1,0:T(8,128)(2,1)} %z_in.1, s32[32,128]{1,0:T(8,128)} %mm_ref.1, s32[16,128]{1,0:T(8,128)} %pm_in.1, bf16[2,256,1024]{2,1,0:T(8,128)(2,1)} %row_w.1, bf16[2,8,128]{2,1,0:T(8,128)(2,1)} %bitcast.5, ...), custom_call_target="tpu_custom_call" | custom-call | tf_op jit(solution)/shard_map/pallas_call | solution.py:717
  486.4 0.0 copy-start
  486.4 3.2 copy.29
  489.6 0.0 copy-done
  489.6 0.8 copy.30
Async XLA Ops:
  486.4 3.2 copy-start
